TPU v7x, 128 devices: a whole 4x4x4 slice. The times are simulated.
128 devices in a mesh: days: 32 (over z, y, core), cols: 4 (over x).
Axes of the slice: x: 4, y: 4, z: 4, core: 2. Of those that a mesh axis runs over, the one named last changes fastest.
Arguments:
- stations: int32 [256, 8], replicated, may hold values from 0 to 127, as said below
- counts: int32 [256], replicated, may hold values from 4 to 8, as said below
- q_cols: bfloat16 [16384, 16384], P(None, ('days', 'cols')), may hold values from -6 to 6, as said below
- glob_solution: float32 [16384], P(('days', 'cols')), may hold values from -6 to 6
- inv_blocks: bfloat16 [256, 4096, 128], P('days', 'cols')
- coupling: bfloat16 [256, 4096, 1024], P('days', 'cols'), may hold values from -0.1875 to 0.1875
- local_rhs: float32 [256, 4096], P('days', 'cols'), may hold values from -6 to 6
Outputs:
- local_solution: float32 [256, 4096], P('days', 'cols')
- cov_diag: float32 [256, 4096], P('days', 'cols')
Inputs may be any that keep to these rules, and one draw needn't show every extreme that they name: `stations`: each day names 8 different blocks, the first counts of them observed; the days of one index of days name one block at most 1 times, and some observed block exactly 1 times. `counts`: the first day of every index of days observes 8 blocks. q_cols equals its transpose exactly.
All inputs are finite; a program needn't handle non-finite values.
Results may differ from a plain program's by a relative error of at most 0.0035.
Values may be sent and summed in bfloat16 or wider, within the bound.
No kernel may reach another device: no remote copies, remote signals or barrier semaphores. Data moves between devices by JAX's collectives and lax.ppermute only.
A program may use at most 192 MiB of HBM per device.

v0:
```python
import functools

import jax
import jax.numpy as jnp
from jax import lax
from jax.experimental import pallas as pl
from jax.experimental.pallas import tpu as pltpu
from jax.sharding import PartitionSpec as P


BW = 128
KMAX = 8
QROWS = 112
OROWS = 112
CHUNKS = ((3, "ahead"), (3, "back"), (2, "direct"))


def pack_kernel(shards, day_dev, pos_ref, st_ref, q_ref, out_ref, blocks, items, in_sem, out_sem):
    slots = day_dev * KMAX

    def copies(shard):
        pos = pos_ref[shard]
        day = pos // KMAX
        slot = pos % KMAX
        made = []
        for n in range(4):
            other = st_ref[shard * slots + day * KMAX + (slot + n + 1) % KMAX]
            rows = pl.ds(pl.multiple_of(other * BW, BW), BW)
            made.append(pltpu.make_async_copy(q_ref.at[rows, :], blocks.at[shard, n], in_sem.at[shard, n]))
        return made

    def out_copy(shard):
        return pltpu.make_async_copy(items.at[shard], out_ref.at[shard], out_sem.at[shard])

    @pl.loop(0, shards)
    def _(shard):
        @pl.when(pos_ref[shard] >= 0)
        def _():
            for copy in copies(shard):
                copy.start()

    @pl.loop(0, shards)
    def _(shard):
        @pl.when(pos_ref[shard] >= 0)
        def _():
            for copy in copies(shard):
                copy.wait()
            upper = (pos_ref[shard] % KMAX) < KMAX // 2
            half = blocks[shard, 3]
            lane = lax.broadcasted_iota(jnp.int32, (64, BW), 1)
            turned = pltpu.roll(half[:64].astype(jnp.float32), 64, 1).astype(jnp.bfloat16)
            half = jnp.where(upper, half[:64], jnp.where(lane < 64, turned, half[64:]))
            for q in range(4):
                for n in range(3):
                    items[shard, q, 32 * n : 32 * (n + 1), :] = blocks[shard, n, 32 * q : 32 * (q + 1), :]
                items[shard, q, 96:112, :] = half[16 * q : 16 * (q + 1)]
            out_copy(shard).start()

    @pl.loop(0, shards)
    def _(shard):
        @pl.when(pos_ref[shard] >= 0)
        def _():
            out_copy(shard).wait()


def pack_items(pos, st_flat, q_cols, shards, day_dev):
    return pl.pallas_call(
        functools.partial(pack_kernel, shards, day_dev),
        out_shape=jax.ShapeDtypeStruct((shards, 4, QROWS, BW), jnp.bfloat16),
        grid_spec=pltpu.PrefetchScalarGridSpec(
            num_scalar_prefetch=2,
            grid=(1,),
            in_specs=[pl.BlockSpec(memory_space=pl.ANY)],
            out_specs=pl.BlockSpec(memory_space=pl.ANY),
            scratch_shapes=[
                pltpu.VMEM((shards, 4, BW, BW), jnp.bfloat16),
                pltpu.VMEM((shards, 4, QROWS, BW), jnp.bfloat16),
                pltpu.SemaphoreType.DMA((shards, 4)),
                pltpu.SemaphoreType.DMA((shards,)),
            ],
        ),
        cost_estimate=pl.CostEstimate(flops=5_000_000, bytes_accessed=8_000_000, transcendentals=0),
        name="pack",
    )(pos, st_flat, q_cols)


def own_kernel(me_ref, diag_ref, glob_ref, own_ref):
    diag = diag_ref[...]
    lane32 = lax.broadcasted_iota(jnp.int32, (32, BW), 1)
    rolled = pltpu.roll(diag[64:96].astype(jnp.float32), 64, 1).astype(jnp.bfloat16)
    own_ref[0:64, :] = diag[:64]
    own_ref[64:96, :] = jnp.where(lane32 < 64, rolled, diag[96:])
    own_ref[96:112, :] = jnp.broadcast_to(glob_ref[...], (16, BW)).astype(jnp.bfloat16)


def own_block(owner, q_cols, glob_row):
    return pl.pallas_call(
        own_kernel,
        out_shape=jax.ShapeDtypeStruct((OROWS, BW), jnp.bfloat16),
        grid_spec=pltpu.PrefetchScalarGridSpec(
            num_scalar_prefetch=1,
            grid=(1,),
            in_specs=[
                pl.BlockSpec((BW, BW), lambda i, me: (me[0], 0)),
                pl.BlockSpec((1, BW), lambda i, me: (0, 0)),
            ],
            out_specs=pl.BlockSpec((OROWS, BW), lambda i, me: (0, 0)),
        ),
        cost_estimate=pl.CostEstimate(flops=100_000, bytes_accessed=100_000, transcendentals=0),
        name="own_block",
    )(owner, q_cols, glob_row)


def gmat_kernel(cnt_ref, inv_ref, coup_ref, g_ref, dinv_ref):
    count = cnt_ref[pl.program_id(0)]
    rows, span = coup_ref.shape[1:]
    lane = lax.broadcasted_iota(jnp.int32, (BW, BW), 1)
    row = lax.broadcasted_iota(jnp.int32, (BW, BW), 0)
    mask = (lax.broadcasted_iota(jnp.int32, (1, span), 1) // BW) < count
    for g in range(rows // BW):
        part = slice(g * BW, (g + 1) * BW)
        inv_g = inv_ref[0, part, :]
        full = jnp.dot(inv_g, coup_ref[0, part, :], preferred_element_type=jnp.float32)
        g_ref[0, part, :] = jnp.where(mask, full, 0.0).astype(jnp.bfloat16)
        inv_f = inv_g.astype(jnp.float32)
        dinv_ref[0, g : g + 1, :] = jnp.sum(jnp.where(lane == row, inv_f, 0.0), axis=0, keepdims=True)


def gmat_call(counts, inv_blocks, coupling):
    days, rows, span = coupling.shape
    groups = rows // BW
    return pl.pallas_call(
        gmat_kernel,
        out_shape=(
            jax.ShapeDtypeStruct((days, rows, span), jnp.bfloat16),
            jax.ShapeDtypeStruct((days, groups, BW), jnp.float32),
        ),
        grid_spec=pltpu.PrefetchScalarGridSpec(
            num_scalar_prefetch=1,
            grid=(days,),
            in_specs=[
                pl.BlockSpec((1, rows, BW), lambda i, *_: (i, 0, 0)),
                pl.BlockSpec((1, rows, span), lambda i, *_: (i, 0, 0)),
            ],
            out_specs=[
                pl.BlockSpec((1, rows, span), lambda i, *_: (i, 0, 0)),
                pl.BlockSpec((1, groups, BW), lambda i, *_: (i, 0, 0)),
            ],
        ),
        cost_estimate=pl.CostEstimate(
            flops=8 * days * rows * span * BW, bytes_accessed=days * rows * span * 4, transcendentals=0
        ),
        name="gmat",
    )(counts, inv_blocks, coupling)


def solve_kernel(cnt_ref, inv_ref, coup_ref, rhs_ref, x_ref, sol_ref):
    count = cnt_ref[pl.program_id(0)]
    rows = coup_ref.shape[1]
    groups = rows // BW
    rhs_t = rhs_ref[0].T
    lane = lax.broadcasted_iota(jnp.int32, (BW, BW), 1)
    x_row = [jnp.where(k < count, x_ref[k, 0:1, :].astype(jnp.float32), 0.0) for k in range(KMAX)]
    solved = jnp.zeros((BW, BW), jnp.float32)
    for g in range(groups):
        part = slice(g * BW, (g + 1) * BW)
        acc = coup_ref[0, part, 0:BW].astype(jnp.float32) * x_row[0]
        for k in range(1, KMAX):
            acc += coup_ref[0, part, k * BW : (k + 1) * BW].astype(jnp.float32) * x_row[k]
        dots = jnp.sum(acc, axis=1, keepdims=True)
        resid = rhs_t[:, g : g + 1] - dots
        resid = jnp.where(lane == g, resid, 0.0).astype(jnp.bfloat16)
        solved += jnp.dot(inv_ref[0, part, :], resid, preferred_element_type=jnp.float32)
    sol_ref[0] = solved.T[:groups]


def solve_call(counts, inv_blocks, coupling, rhs, diags):
    days, rows, span = coupling.shape
    groups = rows // BW
    return pl.pallas_call(
        solve_kernel,
        out_shape=jax.ShapeDtypeStruct((days, groups, BW), jnp.float32),
        grid_spec=pltpu.PrefetchScalarGridSpec(
            num_scalar_prefetch=1,
            grid=(days,),
            in_specs=[
                pl.BlockSpec((1, rows, BW), lambda i, *_: (i, 0, 0)),
                pl.BlockSpec((1, rows, span), lambda i, *_: (i, 0, 0)),
                pl.BlockSpec((1, groups, BW), lambda i, *_: (i, 0, 0)),
                pl.BlockSpec((KMAX, 16, BW), lambda i, *_: (i, OROWS // 16 - 1, 0)),
            ],
            out_specs=pl.BlockSpec((1, groups, BW), lambda i, *_: (i, 0, 0)),
        ),
        cost_estimate=pl.CostEstimate(
            flops=4 * days * rows * span * BW, bytes_accessed=days * rows * span * 2, transcendentals=0
        ),
        name="solve",
    )(counts, inv_blocks, coupling, rhs, diags)


def collect_kernel(chunks, st_ref, got_ref, *refs):
    n_out = len(chunks)
    outs = refs[:n_out]
    buf, in_sem, out_sem = refs[n_out:]
    slots = buf.shape[0]

    def copy_in(p):
        return pltpu.make_async_copy(got_ref.at[st_ref[p]], buf.at[p], in_sem.at[p])

    @pl.loop(0, slots)
    def _(p):
        copy_in(p).start()

    made = []
    first = 0
    for n, (days, _) in enumerate(chunks):
        here = slice(first * KMAX, (first + days) * KMAX)

        @pl.loop(first * KMAX, (first + days) * KMAX)
        def _(p):
            copy_in(p).wait()

        copy = pltpu.make_async_copy(buf.at[here], outs[n], out_sem.at[n])
        copy.start()
        made.append(copy)
        first += days
    for copy in made:
        copy.wait()


def collect(my_st, got):
    slots = my_st.shape[0]
    shapes = [(days * KMAX, QROWS, BW) for days, _ in CHUNKS]
    any_spec = pl.BlockSpec(memory_space=pl.ANY)
    return pl.pallas_call(
        functools.partial(collect_kernel, CHUNKS),
        out_shape=tuple(jax.ShapeDtypeStruct(shape, got.dtype) for shape in shapes),
        grid_spec=pltpu.PrefetchScalarGridSpec(
            num_scalar_prefetch=1,
            grid=(1,),
            in_specs=[any_spec],
            out_specs=[any_spec] * len(shapes),
            scratch_shapes=[
                pltpu.VMEM((slots, QROWS, BW), got.dtype),
                pltpu.SemaphoreType.DMA((slots,)),
                pltpu.SemaphoreType.DMA((len(shapes),)),
            ],
        ),
        cost_estimate=pl.CostEstimate(flops=1_000_000, bytes_accessed=4_000_000, transcendentals=0),
        name="collect",
    )(my_st, got)


def diag_pick_kernel(st_ref, all_ref, out_ref, buf, in_sem, out_sem):
    slots = buf.shape[0]

    def copy_in(p):
        return pltpu.make_async_copy(all_ref.at[st_ref[p]], buf.at[p], in_sem.at[p])

    @pl.loop(0, slots)
    def _(p):
        copy_in(p).start()

    @pl.loop(0, slots)
    def _(p):
        copy_in(p).wait()

    copy = pltpu.make_async_copy(buf, out_ref, out_sem.at[0])
    copy.start()
    copy.wait()


def diag_pick(my_st, blocks):
    slots = my_st.shape[0]
    any_spec = pl.BlockSpec(memory_space=pl.ANY)
    return pl.pallas_call(
        diag_pick_kernel,
        out_shape=jax.ShapeDtypeStruct((slots, OROWS, BW), blocks.dtype),
        grid_spec=pltpu.PrefetchScalarGridSpec(
            num_scalar_prefetch=1,
            grid=(1,),
            in_specs=[any_spec],
            out_specs=any_spec,
            scratch_shapes=[
                pltpu.VMEM((slots, OROWS, BW), blocks.dtype),
                pltpu.SemaphoreType.DMA((slots,)),
                pltpu.SemaphoreType.DMA((1,)),
            ],
        ),
        cost_estimate=pl.CostEstimate(flops=1_000_000, bytes_accessed=4_000_000, transcendentals=0),
        name="diag_pick",
    )(my_st, blocks)


def accumulate(g_ref, weights, window, depth, base_ref, out_ref):
    rows = g_ref.shape[1]
    block = 512
    for r in range(rows // block):
        here = slice(r * block, (r + 1) * block)
        acc = jnp.zeros((block, BW), jnp.float32)
        for j in range(KMAX // 2):
            begin = (2 * j + window) % KMAX
            end = min(begin + depth, KMAX)
            left = g_ref[0, here, begin * BW : end * BW]
            if end - begin < depth:
                left = jnp.concatenate([left, g_ref[0, here, : (depth - end + begin) * BW]], axis=1)
            h = jnp.dot(left, weights[j], preferred_element_type=jnp.float32)
            prod = h * g_ref[0, here, j * 2 * BW : (j + 1) * 2 * BW].astype(jnp.float32)
            acc += prod[:, :BW] + prod[:, BW:]
        for b in range(block // BW):
            g = r * (block // BW) + b
            total = jnp.sum(acc[b * BW : (b + 1) * BW].T, axis=0, keepdims=True)
            out_ref[0, g : g + 1, :] = base_ref[0, g : g + 1, :] + 2.0 * total


def diag_kernel(g_ref, base_ref, own_ref, out_ref, weights):
    @pl.when(pl.program_id(0) == 0)
    def _():
        weights[...] = jnp.zeros_like(weights)

    lane64 = lax.broadcasted_iota(jnp.int32, (64, BW), 1)
    for k in range(KMAX):
        j, low = k // 2, (k % 2) * BW
        lanes = slice(low, low + BW)
        top = own_ref[k, 0:64, :].astype(jnp.float32)
        corner = own_ref[k, 64:96, :].astype(jnp.float32)
        bottom = jnp.concatenate([pltpu.roll(corner, 64, 1), corner], axis=0)
        weights[j, low : low + 64, lanes] = jnp.where(lane64 < 64, 0.5 * top, top).astype(jnp.bfloat16)
        weights[j, low + 64 : low + 128, lanes] = jnp.where(lane64 >= 64, 0.5 * bottom, 0.0).astype(jnp.bfloat16)
    accumulate(g_ref, weights, 0, 2, base_ref, out_ref)


def diag_call(gmat, dinv, diags):
    days, rows, span = gmat.shape
    groups = rows // BW
    return pl.pallas_call(
        diag_kernel,
        out_shape=jax.ShapeDtypeStruct((days, groups, BW), jnp.float32),
        grid_spec=pltpu.PrefetchScalarGridSpec(
            num_scalar_prefetch=0,
            grid=(days,),
            in_specs=[
                pl.BlockSpec((1, rows, span), lambda i: (i, 0, 0)),
                pl.BlockSpec((1, groups, BW), lambda i: (i, 0, 0)),
                pl.BlockSpec((KMAX, OROWS, BW), lambda i: (i, 0, 0)),
            ],
            out_specs=pl.BlockSpec((1, groups, BW), lambda i: (i, 0, 0)),
            scratch_shapes=[pltpu.VMEM((KMAX // 2, 2 * BW, 2 * BW), jnp.bfloat16)],
        ),
        cost_estimate=pl.CostEstimate(
            flops=2 * days * rows * span * 2 * BW, bytes_accessed=days * rows * span * 2, transcendentals=0
        ),
        name="diag",
    )(gmat, dinv, diags)


def cov_kernel(lengths, me_ref, g_ref, base_ref, *refs):
    n_in = 4 * len(lengths) + 1
    out_ref, items, weights, sems = refs[n_in:]
    step = pl.program_id(0)
    me = me_ref[0]
    total_days = sum(lengths)
    quad = KMAX // 2

    def copies(chunk, day, slot):
        made = []
        for n, away in enumerate((0, 3, 1, 2)):
            ref = refs[4 * chunk + n]
            made.append(
                pltpu.make_async_copy(
                    ref.at[pl.ds(day * KMAX, KMAX)], items.at[slot, lax.rem(me + away, 4)], sems.at[slot, n]
                )
            )
        return made

    def start(day, slot):
        first = 0
        for chunk, length in enumerate(lengths):

            @pl.when((day >= first) & (day < first + length))
            def _(chunk=chunk, first=first):
                for copy in copies(chunk, day - first, slot):
                    copy.start()

            first += length

    @pl.when(step == 0)
    def _():
        weights[...] = jnp.zeros_like(weights)
        start(step, 0)

    slot = lax.rem(step, 2)
    for copy in copies(0, 0, slot):
        copy.wait()

    @pl.when(step + 1 < total_days)
    def _():
        start(step + 1, 1 - slot)

    lane64 = lax.broadcasted_iota(jnp.int32, (64, BW), 1)
    for k in range(KMAX):
        j, e = k // 2, k % 2
        lanes = slice(e * BW, (e + 1) * BW)
        for n in range(3):
            low = (e + n) * BW
            for q in range(4):
                weights[j, low + 32 * q : low + 32 * (q + 1), lanes] = items[slot, q, k, 32 * n : 32 * (n + 1), :]
        far = jnp.concatenate([items[slot, q, k, 96:112, :] for q in range(4)], axis=0)
        low = (e + 3) * BW
        if k < quad:
            weights[j, low : low + 64, lanes] = far
        else:
            far = far.astype(jnp.float32)
            left = jnp.where(lane64 >= 64, pltpu.roll(far, 64, 1), 0.0)
            weights[j, low : low + 64, lanes] = left.astype(jnp.bfloat16)
            weights[j, low + 64 : low + 128, lanes] = jnp.where(lane64 >= 64, far, 0.0).astype(jnp.bfloat16)
    accumulate(g_ref, weights, 1, 5, base_ref, out_ref)


def cov_call(me, gmat, base, chunks, last, first):
    rows, span = gmat.shape[1:]
    groups = rows // BW
    lengths = tuple(chunk[0] for chunk in chunks)
    days = sum(lengths)
    depth = 5 * BW
    arrays = [array for chunk in chunks for array in chunk[1:]] + [last]
    return pl.pallas_call(
        functools.partial(cov_kernel, lengths),
        out_shape=jax.ShapeDtypeStruct((days, groups, BW), jnp.float32),
        grid_spec=pltpu.PrefetchScalarGridSpec(
            num_scalar_prefetch=1,
            grid=(days,),
            in_specs=[
                pl.BlockSpec((1, rows, span), lambda i, *_: (i + first, 0, 0)),
                pl.BlockSpec((1, groups, BW), lambda i, *_: (i + first, 0, 0)),
            ]
            + [pl.BlockSpec(memory_space=pl.ANY)] * len(arrays),
            out_specs=pl.BlockSpec((1, groups, BW), lambda i, *_: (i, 0, 0)),
            scratch_shapes=[
                pltpu.VMEM((2, 4, KMAX, QROWS, BW), jnp.bfloat16),
                pltpu.VMEM((KMAX // 2, depth, 2 * BW), jnp.bfloat16),
                pltpu.SemaphoreType.DMA((2, 4)),
            ],
        ),
        cost_estimate=pl.CostEstimate(
            flops=2 * days * rows * span * depth, bytes_accessed=days * rows * span * 2, transcendentals=0
        ),
    )(me, gmat, base, *arrays)


def local(stations, counts, q_cols, glob_solution, inv_blocks, coupling, local_rhs):
    shards = lax.axis_size("days")
    ncols = lax.axis_size("cols")
    me = lax.axis_index("cols")
    my_shard = lax.axis_index("days")
    owner = my_shard * ncols + me
    day_dev, rows, _ = inv_blocks.shape
    slots = day_dev * KMAX
    groups = rows // BW

    shard_st = stations.reshape(shards, slots)
    order = jnp.arange(slots, dtype=jnp.int32)
    pos = jnp.max(jnp.where(shard_st == owner, order[None, :], -1), axis=1)
    st_flat = stations.reshape(-1)
    glob_row = glob_solution.reshape(1, BW)
    my_st = lax.dynamic_slice_in_dim(stations, my_shard * day_dev, day_dev, 0).reshape(slots)
    my_counts = lax.dynamic_slice_in_dim(counts, my_shard * day_dev, day_dev, 0)
    rhs = local_rhs.reshape(day_dev, groups, BW)
    perms = {
        "ahead": [(i, (i + 1) % ncols) for i in range(ncols)],
        "back": [(i, (i - 1) % ncols) for i in range(ncols)],
        "direct": [(i, (i + 2) % ncols) for i in range(ncols)],
    }
    me = me.reshape(1)

    own = own_block(owner.reshape(1), q_cols, glob_row)
    own_blocks = lax.all_gather(own, ("days", "cols"), axis=0)
    items = pack_items(pos, st_flat, q_cols, shards, day_dev)
    got = lax.all_to_all(
        items.reshape(shards * ncols, QROWS, BW), ("days", "cols"), split_axis=0, concat_axis=0, tiled=True
    )
    gmat, dinv = gmat_call(my_counts, inv_blocks, coupling)
    owns = collect(my_st, got)
    chunks = []
    for (days, way), own in zip(CHUNKS, owns):
        behind = lax.ppermute(own, "cols", perms["ahead"])
        before = lax.ppermute(own, "cols", perms["back"])
        far = lax.ppermute({"ahead": behind, "back": before, "direct": own}[way], "cols", perms[way])
        chunks.append((days, own, behind, before, far))
    diags = diag_pick(my_st, own_blocks)
    solved = solve_call(my_counts, inv_blocks, coupling, rhs, diags)
    base = diag_call(gmat, dinv, diags)
    early = sum(chunk[0] for chunk in chunks[:2])
    cov_0 = cov_call(me, gmat, base, chunks[:2], base, 0)
    cov_1 = cov_call(me, gmat, base, chunks[2:], cov_0, early)
    cov = jnp.concatenate([cov_0, cov_1], axis=0)
    return solved.reshape(day_dev, rows), cov.reshape(day_dev, rows)


def solution(mesh):
    return jax.shard_map(
        local,
        mesh=mesh,
        in_specs=(
            P(),
            P(),
            P(None, ("days", "cols")),
            P(("days", "cols")),
            P("days", "cols", None),
            P("days", "cols", None),
            P("days", "cols"),
        ),
        out_specs=(P("days", "cols"), P("days", "cols")),
        check_vma=False,
    )
```

profile of v0, /device:TPU:0, one launch (start us, length us, event | category | flops | bytes accessed | tf_op | source)
XLA Modules:
  0.0 185.0 jit_solution(18150211577986049772)
XLA Ops:
  7.2 0.0 copy-start.5
  7.2 0.0 all-gather.3.cloned.1.call-start
  7.2 1.4 own_block.1
  8.7 0.0 all-gather.3.cloned.1.call-update
  8.7 0.1 broadcast_in_dim.25
  8.8 0.0 copy-done.5
  8.9 0.1 copy.11
  9.0 0.1 reduce_max.14
  9.1 0.7 reshape.41.st_ref
  9.8 0.6 reduce_max.18.pos_ref
  10.4 5.4 %pack.1 = bf16[32,4,112,128]{3,2,1,0:T(8,128)(2,1)} custom-call(s32[32]{0:T(128)} %reduce_max.18.pos_ref, s32[2048]{0:T(1024)} %reshape.41.st_ref, bf16[16384,128]{1,0:T(8,128)(2,1)} %q_ref.1), custom_call_target="tpu_custom_call" | custom-call | flops 5000000 | bytes 8000000 | tf_op jit(solution)/shard_map/pack/pallas_call | solution.py:67
  15.8 0.0 copy-start.6
  15.8 0.0 copy-start.9
  15.8 11.9 %all-to-all-start = ((bf16[128,112,128]{2,1,0:T(8,128)(2,1)}), bf16[128,112,128]{2,1,0:T(8,128)(2,1)}, u32[]{:S(2)}, u32[]{:S(2)}) async-start(bf16[128,112,128]{2,1,0:T(8,128)(2,1)} %bitcast.20), calls=%async_computation | async-start | bytes 7340032 | tf_op jit(solution)/shard_map/all_to_all | solution.py:479
  27.8 0.0 copy-done.6
  27.8 0.6 copy.20
  28.4 0.0 copy-done.9
  28.4 0.6 dynamic_slice.6.cnt_ref
  29.0 0.1 constant_dynamic-slice_fusion
  29.1 0.1 copy.10
  29.2 0.6 reshape.36.st_ref
  29.8 45.3 %all-to-all-done.got_ref = bf16[128,112,128]{2,1,0:T(8,128)(2,1)} async-done(((bf16[128,112,128]{2,1,0:T(8,128)(2,1)}), bf16[128,112,128]{2,1,0:T(8,128)(2,1)}, u32[]{:S(2)}, u32[]{:S(2)}) %all-to-all-start) | async-done | bytes 3670048 | tf_op jit(solution)/shard_map/all_to_all | solution.py:479
  75.1 3.6 %collect.1 = (bf16[24,112,128]{2,1,0:T(8,128)(2,1)}, bf16[24,112,128]{2,1,0:T(8,128)(2,1)}, bf16[16,112,128]{2,1,0:T(8,128)(2,1)}) custom-call(s32[64]{0:T(128)} %reshape.36.st_ref, bf16[128,112,128]{2,1,0:T(8,128)(2,1)} %all-to-all-done.got_ref), custom_call_target="tpu_custom_call" | custom-call | flops 1000000 | bytes 4000000 | tf_op jit(solution)/shard_map/collect/pallas_call | solution.py:235
  78.7 1.1 collective-permute-start
  79.8 0.0 copy-start.7
  79.8 0.0 copy-start.8
  79.8 0.0 copy-start
  79.8 2.2 %collective-permute-start.4 = (bf16[24,112,128]{2,1,0:T(8,128)(2,1)}, bf16[24,112,128]{2,1,0:T(8,128)(2,1)}, u32[]{:S(2)}, u32[]{:S(2)}) collective-permute-start(bf16[24,112,128]{2,1,0:T(8,128)(2,1)} %get-tuple-element.10.refs_4_), channel_id=1, source_target_pairs={{0,3},{1,0},{2,1},{3,2},{4,7},{5,4},{6,5},{7,6},{8,11},{9,8},{10,9... | collective-permute-start | bytes 2064392 | tf_op jit(solution)/shard_map/ppermute | solution.py:487
  82.0 16.9 %gmat.1 = (bf16[8,1024,1024]{2,1,0:T(8,128)(2,1)}, f32[8,8,128]{2,1,0:T(8,128)}) custom-call(s32[8]{0:T(128)} %dynamic_slice.6.cnt_ref, bf16[8,1024,128]{2,1,0:T(8,128)(2,1)} %inv_ref.3, bf16[8,1024,1024]{2,1,0:T(8,128)(2,1)} %coup_ref.3), custom_call_target="tpu_custom_call" | custom-call | flops 8589934592 | bytes 33554432 | tf_op jit(solution)/shard_map/gmat/pallas_call | solution.py:132
  98.9 0.0 copy-done.7
  98.9 0.8 collective-permute-start.1
  99.7 0.0 copy-done.8
  99.7 1.2 collective-permute-start.3
  100.9 0.0 copy-done
  100.9 0.1 collective-permute-start.6
  101.0 1.9 %collective-permute-done.refs_1_ = bf16[24,112,128]{2,1,0:T(8,128)(2,1)} collective-permute-done((bf16[24,112,128]{2,1,0:T(8,128)(2,1)}, bf16[24,112,128]{2,1,0:T(8,128)(2,1)}, u32[]{:S(2)}, u32[]{:S(2)}) %collective-permute-start) | collective-permute-done | bytes 688160 | tf_op jit(solution)/shard_map/ppermute | solution.py:486
  102.9 0.0 collective-permute-start.2
  102.9 0.0 collective-permute-done.4.refs_6_
  102.9 3.7 %collective-permute-start.5 = (bf16[24,112,128]{2,1,0:T(8,128)(2,1)}, bf16[24,112,128]{2,1,0:T(8,128)(2,1)}, u32[]{:S(2)}, u32[]{:S(2)}) collective-permute-start(bf16[24,112,128]{2,1,0:T(8,128)(2,1)} %collective-permute-done.4.refs_6_), channel_id=1, source_target_pairs={{0,3},{1,0},{2,1},{3,2},{4,7},{5,4},{6,5},{7,6},{8,11},{9,8},{10,9... | collective-permute-start | bytes 2064392 | tf_op jit(solution)/shard_map/ppermute | solution.py:488
  106.6 0.0 all-gather.3.cloned.1.call-done
  106.6 4.0 %diag_pick.1.x_ref.own_ref = bf16[64,112,128]{2,1,0:T(8,128)(2,1)} custom-call(s32[64]{0:T(128)} %reshape.36.st_ref, bf16[128,112,128]{2,1,0:T(8,128)(2,1)} %bitcast.21), custom_call_target="tpu_custom_call" | custom-call | flops 1000000 | bytes 4000000 | tf_op jit(solution)/shard_map/diag_pick/pallas_call | solution.py:276
  110.6 13.3 %solve.1 = f32[8,8,128]{2,1,0:T(8,128)} custom-call(s32[8]{0:T(128)} %dynamic_slice.6.cnt_ref, bf16[8,1024,128]{2,1,0:T(8,128)(2,1)} %inv_ref.3, bf16[8,1024,1024]{2,1,0:T(8,128)(2,1)} %coup_ref.3, f32[8,8,128]{2,1,0:T(8,128)} %bitcast.22, bf16[64,112,128]{2,1,0:T(8,128)(2,1)} %diag_pick.1.x_ref.own_ref), custom_call_target="tpu_custom_call" | custom-call | flops 4294967296 | bytes 16777216 | tf_op jit(solution)/shard_map/solve/pallas_call | solution.py:180
  123.9 1.4 copy.19
  125.3 11.9 %diag.1.base_ref.refs_8_ = f32[8,8,128]{2,1,0:T(8,128)} custom-call(bf16[8,1024,1024]{2,1,0:T(8,128)(2,1)} %get-tuple-element.7.g_ref, f32[8,8,128]{2,1,0:T(8,128)} %get-tuple-element.8.base_ref, bf16[64,112,128]{2,1,0:T(8,128)(2,1)} %diag_pick.1.x_ref.own_ref), custom_call_target="tpu_custom_call" | custom-call | flops 4294967296 | bytes 16777216 | tf_op jit(solution)/shard_map/diag/pallas_call | solution.py:336
  137.2 0.0 collective-permute-done.1.refs_2_
  137.2 0.0 collective-permute-start.7
  137.2 0.0 collective-permute-done.3.refs_5_
  137.2 0.4 collective-permute-start.8
  137.6 14.4 %collective-permute-done.2.refs_3_ = bf16[24,112,128]{2,1,0:T(8,128)(2,1)} collective-permute-done((bf16[24,112,128]{2,1,0:T(8,128)(2,1)}, bf16[24,112,128]{2,1,0:T(8,128)(2,1)}, u32[]{:S(2)}, u32[]{:S(2)}) %collective-permute-start.2) | collective-permute-done | bytes 688160 | tf_op jit(solution)/shard_map/ppermute | solution.py:488
  152.1 0.0 collective-permute-done.5.refs_7_
  152.1 15.5 %shard_map.86.refs_4_ = f32[6,8,128]{2,1,0:T(8,128)} custom-call(s32[1]{0:T(128)} %bitcast.3.me_ref, bf16[8,1024,1024]{2,1,0:T(8,128)(2,1)} %get-tuple-element.7.g_ref, f32[8,8,128]{2,1,0:T(8,128)} %diag.1.base_ref.refs_8_, bf16[24,112,128]{2,1,0:T(8,128)(2,1)} %get-tuple-element.9.refs_0_, bf16[24,112,128]{2,1,0:T(8,128)(2,1)} %collective-permute-done.refs_1_, ...), custom_call_target="tpu_custom_call" | custom-call | flops 8053063680 | bytes 12582912 | tf_op jit(solution)/shard_map/pallas_call | solution.py:427
  167.6 0.0 copy-start.4
  167.6 0.0 collective-permute-done.6.refs_1_
  167.6 0.0 copy-start.1
  167.6 0.0 collective-permute-done.7.refs_2_
  167.6 0.0 copy-start.2
  167.6 0.0 collective-permute-done.8.refs_3_
  167.7 0.7 copy-done.1
  168.4 0.2 copy-done.2
  168.6 0.8 copy-done.3
  169.3 7.5 %shard_map.87 = f32[2,8,128]{2,1,0:T(8,128)} custom-call(s32[1]{0:T(128)} %bitcast.3.me_ref, bf16[8,1024,1024]{2,1,0:T(8,128)(2,1)} %get-tuple-element.7.g_ref, f32[8,8,128]{2,1,0:T(8,128)} %diag.1.base_ref.refs_8_, bf16[16,112,128]{2,1,0:T(8,128)(2,1)} %get-tuple-element.11.refs_0_, bf16[16,112,128]{2,1,0:T(8,128)(2,1)} %copy-done.1, ...), custom_call_target="tpu_custom_call" | custom-call | flops 2684354560 | bytes 4194304 | tf_op jit(solution)/shard_map/pallas_call | solution.py:427
  176.9 0.0 copy-done.4
  176.9 0.7 maximum_bitcast_fusion
  177.6 0.6 copy.18
  (4 shorter events, 0.0 us)
Async XLA Ops:
  7.2 1.7 copy-start.5
  7.2 99.4 %all-gather.3.cloned.1.call-start = ((), (), s32[]{:S(2)}) async-start(), calls=%async_computation.1 | async-start | bytes 3698688 | tf_op jit(solution)/shard_map/all_gather | solution.py:477
  15.8 12.0 %copy-start.6 = (f32[8,1024]{1,0:T(8,128)S(1)}, f32[8,1024]{1,0:T(8,128)}, u32[]{:S(2)}) copy-start(f32[8,1024]{1,0:T(8,128)} %param.13) | copy-start | bytes 98308
  15.8 12.6 %copy-start.9 = (s32[256]{0:T(256)S(1)}, s32[256]{0:T(256)}, u32[]{:S(2)}) copy-start(s32[256]{0:T(256)} %param.8) | copy-start | bytes 3076
  15.8 59.2 %all-to-all-start = ((bf16[128,112,128]{2,1,0:T(8,128)(2,1)}), bf16[128,112,128]{2,1,0:T(8,128)(2,1)}, u32[]{:S(2)}, u32[]{:S(2)}) async-start(bf16[128,112,128]{2,1,0:T(8,128)(2,1)} %bitcast.20), calls=%async_computation | async-start | bytes 7340032 | tf_op jit(solution)/shard_map/all_to_all | solution.py:479
  78.7 24.2 %collective-permute-start = (bf16[24,112,128]{2,1,0:T(8,128)(2,1)}, bf16[24,112,128]{2,1,0:T(8,128)(2,1)}, u32[]{:S(2)}, u32[]{:S(2)}) collective-permute-start(bf16[24,112,128]{2,1,0:T(8,128)(2,1)} %get-tuple-element.9.refs_0_), channel_id=1, source_target_pairs={{0,1},{1,2},{2,3},{3,0},{4,5},{5,6},{6,7},{7,4},{8,9},{9,10},{10,1... | collective-permute-start | bytes 2064392 | tf_op jit(solution)/shard_map/ppermute | solution.py:486
  79.8 19.1 %copy-start.7 = (bf16[24,112,128]{2,1,0:T(8,128)(2,1)S(1)}, bf16[24,112,128]{2,1,0:T(8,128)(2,1)}, u32[]{:S(2)}) copy-start(bf16[24,112,128]{2,1,0:T(8,128)(2,1)} %get-tuple-element.9.refs_0_) | copy-start | bytes 2064388
  79.8 19.9 %copy-start.8 = (bf16[24,112,128]{2,1,0:T(8,128)(2,1)S(1)}, bf16[24,112,128]{2,1,0:T(8,128)(2,1)}, u32[]{:S(2)}) copy-start(bf16[24,112,128]{2,1,0:T(8,128)(2,1)} %get-tuple-element.10.refs_4_) | copy-start | bytes 2064388
  79.8 21.1 %copy-start = (bf16[16,112,128]{2,1,0:T(8,128)(2,1)S(1)}, bf16[16,112,128]{2,1,0:T(8,128)(2,1)}, u32[]{:S(2)}) copy-start(bf16[16,112,128]{2,1,0:T(8,128)(2,1)} %get-tuple-element.11.refs_0_) | copy-start | bytes 1376260
  79.8 23.1 %collective-permute-start.4 = (bf16[24,112,128]{2,1,0:T(8,128)(2,1)}, bf16[24,112,128]{2,1,0:T(8,128)(2,1)}, u32[]{:S(2)}, u32[]{:S(2)}) collective-permute-start(bf16[24,112,128]{2,1,0:T(8,128)(2,1)} %get-tuple-element.10.refs_4_), channel_id=1, source_target_pairs={{0,3},{1,0},{2,1},{3,2},{4,7},{5,4},{6,5},{7,6},{8,11},{9,8},{10,9... | collective-permute-start | bytes 2064392 | tf_op jit(solution)/shard_map/ppermute | solution.py:487
  98.9 38.3 %collective-permute-start.1 = (bf16[24,112,128]{2,1,0:T(8,128)(2,1)S(1)}, bf16[24,112,128]{2,1,0:T(8,128)(2,1)}, u32[]{:S(2)}, u32[]{:S(2)}) collective-permute-start(bf16[24,112,128]{2,1,0:T(8,128)(2,1)S(1)} %copy-done.7), channel_id=1, source_target_pairs={{0,3},{1,0},{2,1},{3,2},{4,7},{5,4},{6,5},{7,6},{8,11},{9,8},{10,9... | collective-permute-start | bytes 2064392 | tf_op jit(solution)/shard_map/ppermute | solution.py:487
  99.7 37.5 %collective-permute-start.3 = (bf16[24,112,128]{2,1,0:T(8,128)(2,1)S(1)}, bf16[24,112,128]{2,1,0:T(8,128)(2,1)}, u32[]{:S(2)}, u32[]{:S(2)}) collective-permute-start(bf16[24,112,128]{2,1,0:T(8,128)(2,1)S(1)} %copy-done.8), channel_id=1, source_target_pairs={{0,1},{1,2},{2,3},{3,0},{4,5},{5,6},{6,7},{7,4},{8,9},{9,10},{10,1... | collective-permute-start | bytes 2064392 | tf_op jit(solution)/shard_map/ppermute | solution.py:486
  100.9 66.7 %collective-permute-start.6 = (bf16[16,112,128]{2,1,0:T(8,128)(2,1)S(1)}, bf16[16,112,128]{2,1,0:T(8,128)(2,1)S(1)}, u32[]{:S(2)}, u32[]{:S(2)}) collective-permute-start(bf16[16,112,128]{2,1,0:T(8,128)(2,1)S(1)} %copy-done), channel_id=1, source_target_pairs={{0,1},{1,2},{2,3},{3,0},{4,5},{5,6},{6,7},{7,4},{8,9},{9,10},{10,1... | collective-permute-start | bytes 1376264 | tf_op jit(solution)/shard_map/ppermute | solution.py:486
  102.9 49.2 %collective-permute-start.2 = (bf16[24,112,128]{2,1,0:T(8,128)(2,1)}, bf16[24,112,128]{2,1,0:T(8,128)(2,1)}, u32[]{:S(2)}, u32[]{:S(2)}) collective-permute-start(bf16[24,112,128]{2,1,0:T(8,128)(2,1)} %collective-permute-done.refs_1_), channel_id=1, source_target_pairs={{0,1},{1,2},{2,3},{3,0},{4,5},{5,6},{6,7},{7,4},{8,9},{9,10},{10,1... | collective-permute-start | bytes 2064392 | tf_op jit(solution)/shard_map/ppermute | solution.py:488
  102.9 49.2 %collective-permute-start.5 = (bf16[24,112,128]{2,1,0:T(8,128)(2,1)}, bf16[24,112,128]{2,1,0:T(8,128)(2,1)}, u32[]{:S(2)}, u32[]{:S(2)}) collective-permute-start(bf16[24,112,128]{2,1,0:T(8,128)(2,1)} %collective-permute-done.4.refs_6_), channel_id=1, source_target_pairs={{0,3},{1,0},{2,1},{3,2},{4,7},{5,4},{6,5},{7,6},{8,11},{9,8},{10,9... | collective-permute-start | bytes 2064392 | tf_op jit(solution)/shard_map/ppermute | solution.py:488
  137.2 30.4 %collective-permute-start.7 = (bf16[16,112,128]{2,1,0:T(8,128)(2,1)S(1)}, bf16[16,112,128]{2,1,0:T(8,128)(2,1)S(1)}, u32[]{:S(2)}, u32[]{:S(2)}) collective-permute-start(bf16[16,112,128]{2,1,0:T(8,128)(2,1)S(1)} %copy-done), channel_id=1, source_target_pairs={{0,3},{1,0},{2,1},{3,2},{4,7},{5,4},{6,5},{7,6},{8,11},{9,8},{10,9... | collective-permute-start | bytes 1376264 | tf_op jit(solution)/shard_map/ppermute | solution.py:487
  137.2 30.4 %collective-permute-start.8 = (bf16[16,112,128]{2,1,0:T(8,128)(2,1)S(1)}, bf16[16,112,128]{2,1,0:T(8,128)(2,1)S(1)}, u32[]{:S(2)}, u32[]{:S(2)}) collective-permute-start(bf16[16,112,128]{2,1,0:T(8,128)(2,1)S(1)} %copy-done), channel_id=1, source_target_pairs={{0,2},{1,3},{2,0},{3,1},{4,6},{5,7},{6,4},{7,5},{8,10},{9,11},{10,... | collective-permute-start | bytes 1376264 | tf_op jit(solution)/shard_map/ppermute | solution.py:488
  167.6 9.3 %copy-start.4 = (f32[6,8,128]{2,1,0:T(8,128)S(1)}, f32[6,8,128]{2,1,0:T(8,128)}, u32[]{:S(2)}) copy-start(f32[6,8,128]{2,1,0:T(8,128)} %shard_map.86.refs_4_) | copy-start | bytes 73732
  167.6 0.8 copy-start.1
  167.6 0.9 copy-start.2
  168.6 0.8 copy-start.3
Sparse Core Ops, SparseCore 0:
  11.4 92.2 all-gather.2
where the time goes:
time: 186 us; the launch traced here: 185 us
  Pallas kernels  79.6 us (43%)
  waiting for transfers between devices  61.7 us (33%)
  starting transfers between devices  21.5 us (12%)
  between operations  14.2 us (8%)
  local copies, waits for them, and re-layouts  6.73 us (4%)
    all_to_all x1, waiting for transfers between devices, local(): lax.all_to_all(items.reshape(shards * ncols, QROWS, BW), ('days', 'cols')...  45.3 us
    pallas_call x2, Pallas kernels, cov_call(): pl.pallas_call(functools.partial(cov_kernel, lengths), out_shape=jax.Shap...  23 us
    pallas_call x1, Pallas kernels, gmat_call(): pl.pallas_call(gmat_kernel, out_shape=(jax.ShapeDtypeStruct((days, rows,...  16.9 us
    ppermute x3, waiting for transfers between devices, local(): lax.ppermute({'ahead': behind, 'back': before, 'direct': own}[way], 'cols...  14.5 us
    pallas_call x1, Pallas kernels, solve_call(): pl.pallas_call(solve_kernel, out_shape=jax.ShapeDtypeStruct((days, groups...  13.3 us
    all_to_all x1, starting transfers between devices, local(): lax.all_to_all(items.reshape(shards * ncols, QROWS, BW), ('days', 'cols')...  11.9 us
    pallas_call x1, Pallas kernels, diag_call(): pl.pallas_call(diag_kernel, out_shape=jax.ShapeDtypeStruct((days, groups,...  11.9 us
    pallas_call x1, Pallas kernels, pack_items(): pl.pallas_call(functools.partial(pack_kernel, shards, day_dev), out_shape...  5.38 us
  transfers between devices with their start and end apart: 11, of which 3 were waited for; matrix products, arithmetic and copies ran while one was open for 3% of the time, Pallas kernels for 38%

commit v1 on v0

v1 whole, which is shorter than its diff:
```python
import functools

import jax
import jax.numpy as jnp
from jax import lax
from jax.experimental import pallas as pl
from jax.experimental.pallas import tpu as pltpu
from jax.sharding import PartitionSpec as P


BW = 128
KMAX = 8
ROWS = (64, 80)
OFFSETS = ((0, 1), (2, 3, 4))
CHUNKS = (((4, "ahead"), (4, "back")), ((3, "ahead"), (3, "back"), (2, "direct")))


def pack_kernel(part, shards, day_dev, pos_ref, st_ref, q_ref, glob_ref, out_ref, blocks, items, in_sem, out_sem):
    slots = day_dev * KMAX

    def copies(shard):
        pos = pos_ref[shard]
        day = pos // KMAX
        slot = pos % KMAX
        made = []
        for n, off in enumerate(OFFSETS[part]):
            other = st_ref[shard * slots + day * KMAX + (slot + off) % KMAX]
            rows = pl.ds(pl.multiple_of(other * BW, BW), BW)
            made.append(pltpu.make_async_copy(q_ref.at[rows, :], blocks.at[shard, n], in_sem.at[shard, n]))
        return made

    def out_copy(shard):
        return pltpu.make_async_copy(items.at[shard], out_ref.at[shard], out_sem.at[shard])

    @pl.loop(0, shards)
    def _(shard):
        @pl.when(pos_ref[shard] >= 0)
        def _():
            for copy in copies(shard):
                copy.start()

    x_rows = jnp.broadcast_to(glob_ref[...], (8, BW))

    def fill_first(shard):
        diag = blocks[shard, 0]
        lane32 = lax.broadcasted_iota(jnp.int32, (32, BW), 1)
        corner = jnp.where(
            lane32 < 64,
            pltpu.roll(diag[64:96].astype(jnp.float32), 64, 1),
            diag[96:].astype(jnp.float32),
        )
        for q in range(4):
            items[shard, q, 0:32, :] = blocks[shard, 1, 32 * q : 32 * (q + 1), :]
            items[shard, q, 32:48, :] = diag[16 * q : 16 * (q + 1)]
            items[shard, q, 48:64, :] = jnp.concatenate([corner[8 * q : 8 * (q + 1)], x_rows], axis=0).astype(
                jnp.bfloat16
            )

    def fill_second(shard):
        upper = (pos_ref[shard] % KMAX) < KMAX // 2
        half = blocks[shard, 2]
        lane = lax.broadcasted_iota(jnp.int32, (64, BW), 1)
        rolled = pltpu.roll(half[:64].astype(jnp.float32), 64, 1).astype(jnp.bfloat16)
        half = jnp.where(upper, half[:64], jnp.where(lane < 64, rolled, half[64:]))
        for q in range(4):
            for n in range(2):
                items[shard, q, 32 * n : 32 * (n + 1), :] = blocks[shard, n, 32 * q : 32 * (q + 1), :]
            items[shard, q, 64:80, :] = half[16 * q : 16 * (q + 1)]

    @pl.loop(0, shards)
    def _(shard):
        @pl.when(pos_ref[shard] >= 0)
        def _():
            for copy in copies(shard):
                copy.wait()
            (fill_first, fill_second)[part](shard)
            out_copy(shard).start()

    @pl.loop(0, shards)
    def _(shard):
        @pl.when(pos_ref[shard] >= 0)
        def _():
            out_copy(shard).wait()


def pack_items(part, pos, st_flat, q_cols, glob_row, shards, day_dev):
    n_off = len(OFFSETS[part])
    return pl.pallas_call(
        functools.partial(pack_kernel, part, shards, day_dev),
        out_shape=jax.ShapeDtypeStruct((shards, 4, ROWS[part], BW), jnp.bfloat16),
        grid_spec=pltpu.PrefetchScalarGridSpec(
            num_scalar_prefetch=2,
            grid=(1,),
            in_specs=[
                pl.BlockSpec(memory_space=pl.ANY),
                pl.BlockSpec((1, BW), lambda i, *_: (0, 0)),
            ],
            out_specs=pl.BlockSpec(memory_space=pl.ANY),
            scratch_shapes=[
                pltpu.VMEM((shards, n_off, BW, BW), jnp.bfloat16),
                pltpu.VMEM((shards, 4, ROWS[part], BW), jnp.bfloat16),
                pltpu.SemaphoreType.DMA((shards, n_off)),
                pltpu.SemaphoreType.DMA((shards,)),
            ],
        ),
        cost_estimate=pl.CostEstimate(flops=5_000_000, bytes_accessed=5_000_000, transcendentals=0),
    )(pos, st_flat, q_cols, glob_row)


def gmat_kernel(cnt_ref, inv_ref, coup_ref, g_ref, dinv_ref):
    count = cnt_ref[pl.program_id(0)]
    rows, span = coup_ref.shape[1:]
    lane = lax.broadcasted_iota(jnp.int32, (BW, BW), 1)
    row = lax.broadcasted_iota(jnp.int32, (BW, BW), 0)
    mask = (lax.broadcasted_iota(jnp.int32, (1, span), 1) // BW) < count
    for g in range(rows // BW):
        part = slice(g * BW, (g + 1) * BW)
        inv_g = inv_ref[0, part, :]
        full = jnp.dot(inv_g, coup_ref[0, part, :], preferred_element_type=jnp.float32)
        g_ref[0, part, :] = jnp.where(mask, full, 0.0).astype(jnp.bfloat16)
        inv_f = inv_g.astype(jnp.float32)
        dinv_ref[0, g : g + 1, :] = jnp.sum(jnp.where(lane == row, inv_f, 0.0), axis=0, keepdims=True)


def gmat_call(counts, inv_blocks, coupling):
    days, rows, span = coupling.shape
    groups = rows // BW
    return pl.pallas_call(
        gmat_kernel,
        out_shape=(
            jax.ShapeDtypeStruct((days, rows, span), jnp.bfloat16),
            jax.ShapeDtypeStruct((days, groups, BW), jnp.float32),
        ),
        grid_spec=pltpu.PrefetchScalarGridSpec(
            num_scalar_prefetch=1,
            grid=(days,),
            in_specs=[
                pl.BlockSpec((1, rows, BW), lambda i, *_: (i, 0, 0)),
                pl.BlockSpec((1, rows, span), lambda i, *_: (i, 0, 0)),
            ],
            out_specs=[
                pl.BlockSpec((1, rows, span), lambda i, *_: (i, 0, 0)),
                pl.BlockSpec((1, groups, BW), lambda i, *_: (i, 0, 0)),
            ],
        ),
        cost_estimate=pl.CostEstimate(
            flops=8 * days * rows * span * BW, bytes_accessed=days * rows * span * 4, transcendentals=0
        ),
        name="gmat",
    )(counts, inv_blocks, coupling)


def solve_kernel(cnt_ref, inv_ref, coup_ref, rhs_ref, x_ref, sol_ref):
    count = cnt_ref[pl.program_id(0)]
    rows = coup_ref.shape[1]
    groups = rows // BW
    x8 = jnp.concatenate([x_ref[0, k, 8:9, :].astype(jnp.float32) for k in range(KMAX)], axis=0)
    keep = lax.broadcasted_iota(jnp.int32, (KMAX, BW), 0) < count
    x_t = jnp.where(keep, x8, 0.0).T
    rhs_t = rhs_ref[0].T
    x_col = jnp.concatenate(
        [jnp.broadcast_to(x_t[:, k : k + 1], (BW, BW)) for k in range(KMAX)], axis=0
    ).astype(jnp.bfloat16)
    lane = lax.broadcasted_iota(jnp.int32, (BW, BW), 1)
    dots = jnp.dot(coup_ref[0], x_col, preferred_element_type=jnp.float32)
    solved = jnp.zeros((BW, BW), jnp.float32)
    for g in range(groups):
        part = slice(g * BW, (g + 1) * BW)
        resid = (rhs_t[:, g : g + 1] - dots[part]).astype(jnp.bfloat16)
        resid = jnp.where(lane == g, resid, jnp.zeros_like(resid))
        solved += jnp.dot(inv_ref[0, part, :], resid, preferred_element_type=jnp.float32)
    sol_ref[0] = solved.T[:groups]


def solve_call(counts, inv_blocks, coupling, rhs, x_rows):
    days, rows, span = coupling.shape
    groups = rows // BW
    return pl.pallas_call(
        solve_kernel,
        out_shape=jax.ShapeDtypeStruct((days, groups, BW), jnp.float32),
        grid_spec=pltpu.PrefetchScalarGridSpec(
            num_scalar_prefetch=1,
            grid=(days,),
            in_specs=[
                pl.BlockSpec((1, rows, BW), lambda i, *_: (i, 0, 0)),
                pl.BlockSpec((1, rows, span), lambda i, *_: (i, 0, 0)),
                pl.BlockSpec((1, groups, BW), lambda i, *_: (i, 0, 0)),
                pl.BlockSpec((1, KMAX, 16, BW), lambda i, *_: (i, 0, 0, 0)),
            ],
            out_specs=pl.BlockSpec((1, groups, BW), lambda i, *_: (i, 0, 0)),
        ),
        cost_estimate=pl.CostEstimate(
            flops=4 * days * rows * span * BW, bytes_accessed=days * rows * span * 2, transcendentals=0
        ),
        name="solve",
    )(counts, inv_blocks, coupling, rhs, x_rows)


def collect_kernel(part, chunks, st_ref, got_ref, *refs):
    n_out = len(chunks) + (part == 0)
    outs = refs[:n_out]
    buf, in_sem, out_sem = refs[n_out:]
    slots = buf.shape[0]

    def copy_in(p):
        return pltpu.make_async_copy(got_ref.at[st_ref[p]], buf.at[p], in_sem.at[p])

    @pl.loop(0, slots)
    def _(p):
        copy_in(p).start()

    made = []
    first = 0
    for n, (days, _) in enumerate(chunks):
        here = slice(first * KMAX, (first + days) * KMAX)

        @pl.loop(first * KMAX, (first + days) * KMAX)
        def _(p):
            copy_in(p).wait()

        copy = pltpu.make_async_copy(buf.at[here], outs[n], out_sem.at[n])
        copy.start()
        made.append(copy)
        first += days
    if part == 0:
        copy = pltpu.make_async_copy(buf.at[:, ROWS[0] - 16 :, :], outs[-1], out_sem.at[len(chunks)])
        copy.start()
        made.append(copy)
    for copy in made:
        copy.wait()


def collect(part, my_st, got):
    slots = my_st.shape[0]
    chunks = CHUNKS[part]
    shapes = [(days * KMAX, ROWS[part], BW) for days, _ in chunks]
    if part == 0:
        shapes.append((slots, 16, BW))
    any_spec = pl.BlockSpec(memory_space=pl.ANY)
    return pl.pallas_call(
        functools.partial(collect_kernel, part, chunks),
        out_shape=tuple(jax.ShapeDtypeStruct(shape, got.dtype) for shape in shapes),
        grid_spec=pltpu.PrefetchScalarGridSpec(
            num_scalar_prefetch=1,
            grid=(1,),
            in_specs=[any_spec],
            out_specs=[any_spec] * len(shapes),
            scratch_shapes=[
                pltpu.VMEM((slots, ROWS[part], BW), got.dtype),
                pltpu.SemaphoreType.DMA((slots,)),
                pltpu.SemaphoreType.DMA((len(shapes),)),
            ],
        ),
        cost_estimate=pl.CostEstimate(flops=1_000_000, bytes_accessed=2_500_000, transcendentals=0),
    )(my_st, got)


def cov_kernel(part, lengths, me_ref, g_ref, base_ref, *refs):
    n_in = 4 * len(lengths) + 1
    out_ref, items, weights, sems = refs[n_in:]
    step = pl.program_id(0)
    me = me_ref[0]
    total_days = sum(lengths)
    rows, _ = g_ref.shape[1:]
    quad = KMAX // 2
    window = OFFSETS[part][0]
    depth = OFFSETS[part][-1] + 2 - window

    def copies(chunk, day, slot):
        made = []
        for n, away in enumerate((0, 3, 1, 2)):
            ref = refs[4 * chunk + n]
            made.append(
                pltpu.make_async_copy(
                    ref.at[pl.ds(day * KMAX, KMAX)], items.at[slot, lax.rem(me + away, 4)], sems.at[slot, n]
                )
            )
        return made

    def start(day, slot):
        first = 0
        for chunk, length in enumerate(lengths):

            @pl.when((day >= first) & (day < first + length))
            def _(chunk=chunk, first=first):
                for copy in copies(chunk, day - first, slot):
                    copy.start()

            first += length

    @pl.when(step == 0)
    def _():
        weights[...] = jnp.zeros_like(weights)
        start(step, 0)

    slot = lax.rem(step, 2)
    for copy in copies(0, 0, slot):
        copy.wait()

    @pl.when(step + 1 < total_days)
    def _():
        start(step + 1, 1 - slot)

    lane64 = lax.broadcasted_iota(jnp.int32, (64, BW), 1)
    for k in range(KMAX):
        j, e = k // 2, k % 2
        lanes = slice(e * BW, (e + 1) * BW)
        for at, off in ((0, 1),) if part == 0 else ((0, 2), (32, 3)):
            low = (e + off - window) * BW
            for q in range(4):
                weights[j, low + 32 * q : low + 32 * (q + 1), lanes] = items[slot, q, k, at : at + 32, :]
        if part == 0:
            top = jnp.concatenate([items[slot, q, k, 32:48, :] for q in range(4)], axis=0).astype(jnp.float32)
            corner = jnp.concatenate([items[slot, q, k, 48:64, :].astype(jnp.float32)[:8] for q in range(4)], axis=0)
            low = e * BW
            weights[j, low : low + 64, lanes] = jnp.where(lane64 < 64, 0.5 * top, top).astype(jnp.bfloat16)
            bottom = jnp.concatenate([pltpu.roll(corner, 64, 1), corner], axis=0)
            weights[j, low + 64 : low + 128, lanes] = jnp.where(lane64 >= 64, 0.5 * bottom, 0.0).astype(jnp.bfloat16)
        else:
            far = jnp.concatenate([items[slot, q, k, 64:80, :] for q in range(4)], axis=0)
            low = (e + 4 - window) * BW
            if k < quad:
                weights[j, low : low + 64, lanes] = far
            else:
                far = far.astype(jnp.float32)
                left = jnp.where(lane64 >= 64, pltpu.roll(far, 64, 1), 0.0)
                weights[j, low : low + 64, lanes] = left.astype(jnp.bfloat16)
                weights[j, low + 64 : low + 128, lanes] = jnp.where(lane64 >= 64, far, 0.0).astype(jnp.bfloat16)

    block = 256
    for r in range(rows // block):
        here = slice(r * block, (r + 1) * block)
        acc = jnp.zeros((block, BW), jnp.float32)
        for j in range(quad):
            begin = (2 * j + window) % KMAX
            end = min(begin + depth, KMAX)
            left = g_ref[0, here, begin * BW : end * BW]
            if end - begin < depth:
                left = jnp.concatenate([left, g_ref[0, here, : (depth - end + begin) * BW]], axis=1)
            h = jnp.dot(left, weights[j], preferred_element_type=jnp.float32)
            prod = h * g_ref[0, here, j * 2 * BW : (j + 1) * 2 * BW].astype(jnp.float32)
            acc += prod[:, :BW] + prod[:, BW:]
        for b in range(block // BW):
            g = r * (block // BW) + b
            total = jnp.sum(acc[b * BW : (b + 1) * BW].T, axis=0, keepdims=True)
            out_ref[0, g : g + 1, :] = base_ref[0, g : g + 1, :] + 2.0 * total


def cov_call(part, me, gmat, base, chunks, last, first, base_first):
    rows, span = gmat.shape[1:]
    groups = rows // BW
    lengths = tuple(chunk[0] for chunk in chunks)
    days = sum(lengths)
    depth = (OFFSETS[part][-1] + 2 - OFFSETS[part][0]) * BW
    arrays = [array for chunk in chunks for array in chunk[1:]] + [last]
    return pl.pallas_call(
        functools.partial(cov_kernel, part, lengths),
        out_shape=jax.ShapeDtypeStruct((days, groups, BW), jnp.float32),
        grid_spec=pltpu.PrefetchScalarGridSpec(
            num_scalar_prefetch=1,
            grid=(days,),
            in_specs=[
                pl.BlockSpec((1, rows, span), lambda i, *_: (i + first, 0, 0)),
                pl.BlockSpec((1, groups, BW), lambda i, *_: (i + base_first, 0, 0)),
            ]
            + [pl.BlockSpec(memory_space=pl.ANY)] * len(arrays),
            out_specs=pl.BlockSpec((1, groups, BW), lambda i, *_: (i, 0, 0)),
            scratch_shapes=[
                pltpu.VMEM((2, 4, KMAX, ROWS[part], BW), jnp.bfloat16),
                pltpu.VMEM((KMAX // 2, depth, 2 * BW), jnp.bfloat16),
                pltpu.SemaphoreType.DMA((2, 4)),
            ],
        ),
        cost_estimate=pl.CostEstimate(
            flops=2 * days * rows * span * depth, bytes_accessed=days * rows * span * 2, transcendentals=0
        ),
    )(me, gmat, base, *arrays)


def local(stations, counts, q_cols, glob_solution, inv_blocks, coupling, local_rhs):
    shards = lax.axis_size("days")
    ncols = lax.axis_size("cols")
    me = lax.axis_index("cols")
    my_shard = lax.axis_index("days")
    owner = my_shard * ncols + me
    day_dev, rows, _ = inv_blocks.shape
    slots = day_dev * KMAX
    groups = rows // BW

    shard_st = stations.reshape(shards, slots)
    order = jnp.arange(slots, dtype=jnp.int32)
    pos = jnp.max(jnp.where(shard_st == owner, order[None, :], -1), axis=1)
    st_flat = stations.reshape(-1)
    glob_row = glob_solution.reshape(1, BW)
    my_st = lax.dynamic_slice_in_dim(stations, my_shard * day_dev, day_dev, 0).reshape(slots)
    my_counts = lax.dynamic_slice_in_dim(counts, my_shard * day_dev, day_dev, 0)
    rhs = local_rhs.reshape(day_dev, groups, BW)
    me = me.reshape(1)
    perms = {
        "ahead": [(i, (i + 1) % ncols) for i in range(ncols)],
        "back": [(i, (i - 1) % ncols) for i in range(ncols)],
        "direct": [(i, (i + 2) % ncols) for i in range(ncols)],
    }

    def exchange(part):
        items = pack_items(part, pos, st_flat, q_cols, glob_row, shards, day_dev)
        return lax.all_to_all(
            items.reshape(shards * ncols, ROWS[part], BW),
            ("days", "cols"),
            split_axis=0,
            concat_axis=0,
            tiled=True,
        )

    def ring(part, owns):
        chunks = []
        for (days, way), own in zip(CHUNKS[part], owns):
            behind = lax.ppermute(own, "cols", perms["ahead"])
            before = lax.ppermute(own, "cols", perms["back"])
            far = lax.ppermute({"ahead": behind, "back": before, "direct": own}[way], "cols", perms[way])
            chunks.append((days, own, behind, before, far))
        return chunks

    got_a, got_b = exchange(0), exchange(1)
    gmat, dinv = gmat_call(my_counts, inv_blocks, coupling)
    *owns_a, x_rows = collect(0, my_st, got_a)
    chunks_a = ring(0, owns_a)
    solved = solve_call(my_counts, inv_blocks, coupling, rhs, x_rows.reshape(day_dev, KMAX, 16, BW))
    owns_b = collect(1, my_st, got_b)
    chunks_b = ring(1, owns_b)
    half = cov_call(0, me, gmat, dinv, chunks_a, dinv, 0, 0)
    early = sum(chunk[0] for chunk in chunks_b[:2])
    cov_0 = cov_call(1, me, gmat, half, chunks_b[:2], half, 0, 0)
    cov_1 = cov_call(1, me, gmat, half, chunks_b[2:], cov_0, early, early)
    cov = jnp.concatenate([cov_0, cov_1], axis=0)
    return solved.reshape(day_dev, rows), cov.reshape(day_dev, rows)


def solution(mesh):
    return jax.shard_map(
        local,
        mesh=mesh,
        in_specs=(
            P(),
            P(),
            P(None, ("days", "cols")),
            P(("days", "cols")),
            P("days", "cols", None),
            P("days", "cols", None),
            P("days", "cols"),
        ),
        out_specs=(P("days", "cols"), P("days", "cols")),
        check_vma=False,
    )
```

time: 186 us -> 206 us (1.11)
  starting transfers between devices: 21.5 us -> 34.9 us
  between operations: 14.2 us -> 0.85 us
  waiting for transfers between devices: 61.7 us -> 73.7 us
  local copies, waits for them, and re-layouts: 6.73 us -> 10.1 us
  Pallas kernels: 79.6 us -> 82 us
    ppermute x9 -> x15, starting transfers between devices: 9.5 us -> 18.9 us  [the longest x5 7.88 us: ring(): before = lax.ppermute(own, 'cols', perms['back'])]
    ppermute x9 -> x15, waiting for transfers between devices: 16.4 us -> 23.4 us  [the longest x5 14.2 us: ring(): lax.ppermute({'ahead': behind, 'back': before, 'direct': own}[way], 'cols...]
    all_to_all x1 -> x2, waiting for transfers between devices: 45.3 us -> 50.4 us  [exchange(): lax.all_to_all(items.reshape(shards * ncols, ROWS[part], BW), ('days', 'c...]
    all_to_all x1 -> x2, starting transfers between devices: 11.9 us -> 16 us  [exchange(): lax.all_to_all(items.reshape(shards * ncols, ROWS[part], BW), ('days', 'c...]
    unnamed x24 -> x34, local copies, waits for them, and re-layouts: 4.46 us -> 7.88 us
  transfers between devices with their start and end apart: 11 -> 17, of which waited for: 3 -> 5; matrix products, arithmetic and copies ran while one was open for 3% -> 2% of each run, Pallas kernels for 38% -> 35%
where the time goes in v1:
time: 206 us; the launch traced here: 204 us
  Pallas kernels  82 us (40%)
  waiting for transfers between devices  73.7 us (36%)
  starting transfers between devices  34.9 us (17%)
  local copies, waits for them, and re-layouts  10.1 us (5%)
    all_to_all x2, waiting for transfers between devices, exchange(): lax.all_to_all(items.reshape(shards * ncols, ROWS[part], BW), ('days', 'c...  50.4 us
    pallas_call x3, Pallas kernels, cov_call(): pl.pallas_call(functools.partial(cov_kernel, part, lengths), out_shape=ja...  34.4 us
    pallas_call x1, Pallas kernels, gmat_call(): pl.pallas_call(gmat_kernel, out_shape=(jax.ShapeDtypeStruct((days, rows,...  16.8 us
    all_to_all x2, starting transfers between devices, exchange(): lax.all_to_all(items.reshape(shards * ncols, ROWS[part], BW), ('days', 'c...  16 us
    ppermute x5, waiting for transfers between devices, ring(): lax.ppermute({'ahead': behind, 'back': before, 'direct': own}[way], 'cols...  14.2 us
    pallas_call x1, Pallas kernels, solve_call(): pl.pallas_call(solve_kernel, out_shape=jax.ShapeDtypeStruct((days, groups...  13.9 us
    pallas_call x2, Pallas kernels, pack_items(): pl.pallas_call(functools.partial(pack_kernel, part, shards, day_dev), out...  10.1 us
    ppermute x5, waiting for transfers between devices, ring(): before = lax.ppermute(own, 'cols', perms['back'])  8.07 us
  transfers between devices with their start and end apart: 17, of which 5 were waited for; matrix products, arithmetic and copies ran while one was open for 2% of the time, Pallas kernels for 35%

profile of v1, /device:TPU:0, one launch (start us, length us, event | category | flops | bytes accessed | tf_op | source)
XLA Modules:
  0.0 203.7 jit_solution(16898241588439141908)
XLA Ops:
  0.7 0.1 broadcast_in_dim.25
  0.8 0.8 copy.11
  1.6 0.7 select_reduce_fusion
  2.3 0.1 reduce_max.14
  2.4 0.7 reshape.40.st_ref
  3.1 0.6 reduce_max.18.pos_ref
  3.8 4.9 %shard_map.86 = bf16[32,4,64,128]{3,2,1,0:T(8,128)(2,1)} custom-call(s32[32]{0:T(128)} %reduce_max.18.pos_ref, s32[2048]{0:T(1024)} %reshape.40.st_ref, bf16[16384,128]{1,0:T(8,128)(2,1)} %q_ref.3, f32[1,128]{1,0:T(1,128)} %bitcast.28), custom_call_target="tpu_custom_call" | custom-call | flops 5000000 | bytes 5000000 | tf_op jit(solution)/shard_map/pallas_call | solution.py:88
  8.7 11.4 %all-to-all-start = ((bf16[128,64,128]{2,1,0:T(8,128)(2,1)}), bf16[128,64,128]{2,1,0:T(8,128)(2,1)S(1)}, u32[]{:S(2)}, u32[]{:S(2)}) async-start(bf16[128,64,128]{2,1,0:T(8,128)(2,1)} %bitcast.21), calls=%async_computation | async-start | bytes 4194304 | tf_op jit(solution)/shard_map/all_to_all | solution.py:407
  20.1 5.2 %shard_map.89 = bf16[32,4,80,128]{3,2,1,0:T(8,128)(2,1)} custom-call(s32[32]{0:T(128)} %reduce_max.18.pos_ref, s32[2048]{0:T(1024)} %reshape.40.st_ref, bf16[16384,128]{1,0:T(8,128)(2,1)} %q_ref.3, f32[1,128]{1,0:T(1,128)} %bitcast.29), custom_call_target="tpu_custom_call" | custom-call | flops 5000000 | bytes 5000000 | tf_op jit(solution)/shard_map/pallas_call | solution.py:88
  25.3 24.8 %all-to-all-done.got_ref = bf16[128,64,128]{2,1,0:T(8,128)(2,1)S(1)} async-done(((bf16[128,64,128]{2,1,0:T(8,128)(2,1)}), bf16[128,64,128]{2,1,0:T(8,128)(2,1)S(1)}, u32[]{:S(2)}, u32[]{:S(2)}) %all-to-all-start) | async-done | bytes 2097184 | tf_op jit(solution)/shard_map/all_to_all | solution.py:407
  50.1 1.4 copy-done.1
  51.5 4.7 %all-to-all-start.1 = ((bf16[128,80,128]{2,1,0:T(8,128)(2,1)}), bf16[128,80,128]{2,1,0:T(8,128)(2,1)S(1)}, u32[]{:S(2)}, u32[]{:S(2)}) async-start(bf16[128,80,128]{2,1,0:T(8,128)(2,1)} %bitcast.20), calls=%async_computation.1 | async-start | bytes 5242880 | tf_op jit(solution)/shard_map/all_to_all | solution.py:407
  56.1 0.0 copy-done.7
  56.1 0.1 constant_dynamic-slice_fusion
  56.2 0.1 copy.10
  56.3 0.6 reshape.39.st_ref
  56.9 3.5 %shard_map.87 = (bf16[32,64,128]{2,1,0:T(8,128)(2,1)}, bf16[32,64,128]{2,1,0:T(8,128)(2,1)}, bf16[64,16,128]{2,1,0:T(8,128)(2,1)}) custom-call(s32[64]{0:T(128)} %reshape.39.st_ref, bf16[128,64,128]{2,1,0:T(8,128)(2,1)} %copy-done.1), custom_call_target="tpu_custom_call" | custom-call | flops 1000000 | bytes 2500000 | tf_op jit(solution)/shard_map/pallas_call | solution.py:240
  60.4 0.9 collective-permute-start
  61.3 2.4 %collective-permute-start.1 = (bf16[32,64,128]{2,1,0:T(8,128)(2,1)}, bf16[32,64,128]{2,1,0:T(8,128)(2,1)}, u32[]{:S(2)}, u32[]{:S(2)}) collective-permute-start(bf16[32,64,128]{2,1,0:T(8,128)(2,1)} %get-tuple-element.13.refs_0_), channel_id=1, source_target_pairs={{0,3},{1,0},{2,1},{3,2},{4,7},{5,4},{6,5},{7,6},{8,11},{9,8},{10,9... | collective-permute-start | bytes 1572872 | tf_op jit(solution)/shard_map/ppermute | solution.py:419
  63.7 0.9 collective-permute-start.4
  64.5 0.0 copy-done.14
  64.5 0.6 dynamic_slice.6.cnt_ref
  65.1 1.2 collective-permute-start.3
  66.3 25.5 %all-to-all-done.1.got_ref = bf16[128,80,128]{2,1,0:T(8,128)(2,1)S(1)} async-done(((bf16[128,80,128]{2,1,0:T(8,128)(2,1)}), bf16[128,80,128]{2,1,0:T(8,128)(2,1)S(1)}, u32[]{:S(2)}, u32[]{:S(2)}) %all-to-all-start.1) | async-done | bytes 2621472 | tf_op jit(solution)/shard_map/all_to_all | solution.py:407
  91.8 1.5 copy-done
  93.3 3.4 %shard_map.90 = (bf16[24,80,128]{2,1,0:T(8,128)(2,1)}, bf16[24,80,128]{2,1,0:T(8,128)(2,1)}, bf16[16,80,128]{2,1,0:T(8,128)(2,1)}) custom-call(s32[64]{0:T(128)} %reshape.39.st_ref, bf16[128,80,128]{2,1,0:T(8,128)(2,1)} %copy-done), custom_call_target="tpu_custom_call" | custom-call | flops 1000000 | bytes 2500000 | tf_op jit(solution)/shard_map/pallas_call | solution.py:240
  96.7 0.7 collective-permute-start.6
  97.3 1.1 collective-permute-done.refs_1_
  98.4 1.6 collective-permute-start.10
  100.0 0.0 collective-permute-done.1.refs_2_
  100.0 0.4 collective-permute-start.2
  100.4 8.1 %collective-permute-done.4.refs_6_ = bf16[32,64,128]{2,1,0:T(8,128)(2,1)} collective-permute-done((bf16[32,64,128]{2,1,0:T(8,128)(2,1)}, bf16[32,64,128]{2,1,0:T(8,128)(2,1)}, u32[]{:S(2)}, u32[]{:S(2)}) %collective-permute-start.4) | collective-permute-done | bytes 524320 | tf_op jit(solution)/shard_map/ppermute | solution.py:419
  108.5 2.3 %collective-permute-start.5 = (bf16[32,64,128]{2,1,0:T(8,128)(2,1)}, bf16[32,64,128]{2,1,0:T(8,128)(2,1)S(1)}, u32[]{:S(2)}, u32[]{:S(2)}) collective-permute-start(bf16[32,64,128]{2,1,0:T(8,128)(2,1)} %collective-permute-done.4.refs_6_), channel_id=1, source_target_pairs={{0,3},{1,0},{2,1},{3,2},{4,7},{5,4},{6,5},{7,6},{8,11},{9,8},{10,9... | collective-permute-start | bytes 1572872 | tf_op jit(solution)/shard_map/ppermute | solution.py:420
  110.8 16.8 %gmat.1 = (bf16[8,1024,1024]{2,1,0:T(8,128)(2,1)}, f32[8,8,128]{2,1,0:T(8,128)}) custom-call(s32[8]{0:T(128)} %dynamic_slice.6.cnt_ref, bf16[8,1024,128]{2,1,0:T(8,128)(2,1)} %inv_ref.3, bf16[8,1024,1024]{2,1,0:T(8,128)(2,1)} %coup_ref.3), custom_call_target="tpu_custom_call" | custom-call | flops 8589934592 | bytes 33554432 | tf_op jit(solution)/shard_map/gmat/pallas_call | solution.py:128
  127.6 0.6 copy.20
  128.3 13.9 %solve.1 = f32[8,8,128]{2,1,0:T(8,128)} custom-call(s32[8]{0:T(128)} %dynamic_slice.6.cnt_ref, bf16[8,1024,128]{2,1,0:T(8,128)(2,1)} %inv_ref.3, bf16[8,1024,1024]{2,1,0:T(8,128)(2,1)} %coup_ref.3, f32[8,8,128]{2,1,0:T(8,128)} %bitcast.23, bf16[8,8,16,128]{3,2,1,0:T(8,128)(2,1)} %bitcast.22), custom_call_target="tpu_custom_call" | custom-call | flops 4294967296 | bytes 16777216 | tf_op jit(solution)/shard_map/solve/pallas_call | solution.py:178
  142.2 1.4 copy.19
  143.6 0.0 collective-permute-done.3.refs_5_
  143.6 1.0 collective-permute-start.7
  144.6 0.0 collective-permute-done.6.refs_1_
  144.6 1.0 collective-permute-start.9
  145.6 0.0 collective-permute-done.10.refs_6_
  145.6 0.1 collective-permute-start.12
  145.7 0.0 collective-permute-done.2.refs_3_
  145.7 1.2 collective-permute-start.8
  146.9 0.0 collective-permute-done.5.refs_7_
  146.9 2.1 %collective-permute-start.11 = (bf16[24,80,128]{2,1,0:T(8,128)(2,1)}, bf16[24,80,128]{2,1,0:T(8,128)(2,1)}, u32[]{:S(2)}, u32[]{:S(2)}) collective-permute-start(bf16[24,80,128]{2,1,0:T(8,128)(2,1)} %collective-permute-done.10.refs_6_), channel_id=1, source_target_pairs={{0,3},{1,0},{2,1},{3,2},{4,7},{5,4},{6,5},{7,6},{8,11},{9,8},{10,9... | collective-permute-start | bytes 1474568 | tf_op jit(solution)/shard_map/ppermute | solution.py:420
  149.0 15.6 %shard_map.88.base_ref.refs_8_ = f32[8,8,128]{2,1,0:T(8,128)} custom-call(s32[1]{0:T(128)} %bitcast.3.me_ref, bf16[8,1024,1024]{2,1,0:T(8,128)(2,1)} %get-tuple-element.11.g_ref, f32[8,8,128]{2,1,0:T(8,128)} %get-tuple-element.12.base_ref.refs_8_, bf16[32,64,128]{2,1,0:T(8,128)(2,1)} %get-tuple-element.13.refs_0_, bf16[32,64,128]{2,1,0:T(8,128)(2,1)} %copy-done.9, ...), custom_call_target="tpu_custom_call" | custom-call | flops 6442450944 | bytes 16777216 | tf_op jit(solution)/shard_map/pallas_call | solution.py:356
  164.6 0.0 collective-permute-done.7.refs_2_
  164.6 2.0 collective-permute-start.13
  166.6 0.0 collective-permute-done.9.refs_5_
  166.6 1.2 collective-permute-start.14
  167.9 14.2 %collective-permute-done.8.refs_3_ = bf16[24,80,128]{2,1,0:T(8,128)(2,1)} collective-permute-done((bf16[24,80,128]{2,1,0:T(8,128)(2,1)}, bf16[24,80,128]{2,1,0:T(8,128)(2,1)}, u32[]{:S(2)}, u32[]{:S(2)}) %collective-permute-start.8) | collective-permute-done | bytes 491552 | tf_op jit(solution)/shard_map/ppermute | solution.py:420
  182.0 0.0 collective-permute-done.11.refs_7_
  182.0 12.5 %shard_map.91.refs_4_ = f32[6,8,128]{2,1,0:T(8,128)} custom-call(s32[1]{0:T(128)} %bitcast.3.me_ref, bf16[8,1024,1024]{2,1,0:T(8,128)(2,1)} %get-tuple-element.11.g_ref, f32[8,8,128]{2,1,0:T(8,128)} %shard_map.88.base_ref.refs_8_, bf16[24,80,128]{2,1,0:T(8,128)(2,1)} %get-tuple-element.15.refs_0_, bf16[24,80,128]{2,1,0:T(8,128)(2,1)} %collective-permute-done.6.refs_1_, ...), custom_call_target="tpu_custom_call" | custom-call | flops 6442450944 | bytes 12582912 | tf_op jit(solution)/shard_map/pallas_call | solution.py:356
  194.5 0.0 collective-permute-done.12.refs_1_
  194.6 0.0 collective-permute-done.13.refs_2_
  194.6 0.0 collective-permute-done.14.refs_3_
  194.6 0.7 copy-done.3
  195.3 0.1 copy-done.4
  195.4 0.7 copy-done.5
  196.1 6.3 %shard_map.92 = f32[2,8,128]{2,1,0:T(8,128)} custom-call(s32[1]{0:T(128)} %bitcast.3.me_ref, bf16[8,1024,1024]{2,1,0:T(8,128)(2,1)} %get-tuple-element.11.g_ref, f32[8,8,128]{2,1,0:T(8,128)} %shard_map.88.base_ref.refs_8_, bf16[16,80,128]{2,1,0:T(8,128)(2,1)} %get-tuple-element.17.refs_0_, bf16[16,80,128]{2,1,0:T(8,128)(2,1)} %copy-done.3, ...), custom_call_target="tpu_custom_call" | custom-call | flops 2147483648 | bytes 4194304 | tf_op jit(solution)/shard_map/pallas_call | solution.py:356
  202.4 0.7 maximum_bitcast_fusion
  203.1 0.6 copy.18
  (25 shorter events, 0.1 us)
Async XLA Ops:
  8.7 41.4 %all-to-all-start = ((bf16[128,64,128]{2,1,0:T(8,128)(2,1)}), bf16[128,64,128]{2,1,0:T(8,128)(2,1)S(1)}, u32[]{:S(2)}, u32[]{:S(2)}) async-start(bf16[128,64,128]{2,1,0:T(8,128)(2,1)} %bitcast.21), calls=%async_computation | async-start | bytes 4194304 | tf_op jit(solution)/shard_map/all_to_all | solution.py:407
  50.1 1.4 copy-start.1
  50.1 6.0 %copy-start.7 = (s32[256,8]{0,1:T(8,128)S(1)}, s32[256,8]{0,1:T(8,128)}, u32[]{:S(2)}) copy-start(s32[256,8]{0,1:T(8,128)} %param.7) | copy-start | bytes 24580
  50.1 14.4 %copy-start.14 = (s32[256]{0:T(256)S(1)}, s32[256]{0:T(256)}, u32[]{:S(2)}) copy-start(s32[256]{0:T(256)} %param.8) | copy-start | bytes 3076
  51.5 40.3 %all-to-all-start.1 = ((bf16[128,80,128]{2,1,0:T(8,128)(2,1)}), bf16[128,80,128]{2,1,0:T(8,128)(2,1)S(1)}, u32[]{:S(2)}, u32[]{:S(2)}) async-start(bf16[128,80,128]{2,1,0:T(8,128)(2,1)} %bitcast.20), calls=%async_computation.1 | async-start | bytes 5242880 | tf_op jit(solution)/shard_map/all_to_all | solution.py:407
  60.4 38.0 %collective-permute-start = (bf16[32,64,128]{2,1,0:T(8,128)(2,1)}, bf16[32,64,128]{2,1,0:T(8,128)(2,1)S(1)}, u32[]{:S(2)}, u32[]{:S(2)}) collective-permute-start(bf16[32,64,128]{2,1,0:T(8,128)(2,1)} %get-tuple-element.13.refs_0_), channel_id=1, source_target_pairs={{0,1},{1,2},{2,3},{3,0},{4,5},{5,6},{6,7},{7,4},{8,9},{9,10},{10,1... | collective-permute-start | bytes 1572872 | tf_op jit(solution)/shard_map/ppermute | solution.py:418
  61.3 38.7 %collective-permute-start.1 = (bf16[32,64,128]{2,1,0:T(8,128)(2,1)}, bf16[32,64,128]{2,1,0:T(8,128)(2,1)}, u32[]{:S(2)}, u32[]{:S(2)}) collective-permute-start(bf16[32,64,128]{2,1,0:T(8,128)(2,1)} %get-tuple-element.13.refs_0_), channel_id=1, source_target_pairs={{0,3},{1,0},{2,1},{3,2},{4,7},{5,4},{6,5},{7,6},{8,11},{9,8},{10,9... | collective-permute-start | bytes 1572872 | tf_op jit(solution)/shard_map/ppermute | solution.py:419
  63.7 44.8 %collective-permute-start.4 = (bf16[32,64,128]{2,1,0:T(8,128)(2,1)}, bf16[32,64,128]{2,1,0:T(8,128)(2,1)}, u32[]{:S(2)}, u32[]{:S(2)}) collective-permute-start(bf16[32,64,128]{2,1,0:T(8,128)(2,1)} %get-tuple-element.14.refs_4_), channel_id=1, source_target_pairs={{0,3},{1,0},{2,1},{3,2},{4,7},{5,4},{6,5},{7,6},{8,11},{9,8},{10,9... | collective-permute-start | bytes 1572872 | tf_op jit(solution)/shard_map/ppermute | solution.py:419
  65.1 78.5 %collective-permute-start.3 = (bf16[32,64,128]{2,1,0:T(8,128)(2,1)}, bf16[32,64,128]{2,1,0:T(8,128)(2,1)}, u32[]{:S(2)}, u32[]{:S(2)}) collective-permute-start(bf16[32,64,128]{2,1,0:T(8,128)(2,1)} %get-tuple-element.14.refs_4_), channel_id=1, source_target_pairs={{0,1},{1,2},{2,3},{3,0},{4,5},{5,6},{6,7},{7,4},{8,9},{9,10},{10,1... | collective-permute-start | bytes 1572872 | tf_op jit(solution)/shard_map/ppermute | solution.py:418
  91.8 1.5 copy-start
  96.7 47.9 %collective-permute-start.6 = (bf16[24,80,128]{2,1,0:T(8,128)(2,1)}, bf16[24,80,128]{2,1,0:T(8,128)(2,1)}, u32[]{:S(2)}, u32[]{:S(2)}) collective-permute-start(bf16[24,80,128]{2,1,0:T(8,128)(2,1)} %get-tuple-element.15.refs_0_), channel_id=1, source_target_pairs={{0,1},{1,2},{2,3},{3,0},{4,5},{5,6},{6,7},{7,4},{8,9},{9,10},{10,1... | collective-permute-start | bytes 1474568 | tf_op jit(solution)/shard_map/ppermute | solution.py:418
  98.4 29.2 %copy-start.9 = (bf16[32,64,128]{2,1,0:T(8,128)(2,1)}, bf16[32,64,128]{2,1,0:T(8,128)(2,1)S(1)}, u32[]{:S(2)}) copy-start(bf16[32,64,128]{2,1,0:T(8,128)(2,1)S(1)} %collective-permute-done.refs_1_) | copy-start | bytes 1572868
  98.4 29.2 %copy-start.8 = (f32[8,1024]{1,0:T(8,128)S(1)}, f32[8,1024]{1,0:T(8,128)}, u32[]{:S(2)}) copy-start(f32[8,1024]{1,0:T(8,128)} %param.13) | copy-start | bytes 98308
  98.4 47.2 %collective-permute-start.10 = (bf16[24,80,128]{2,1,0:T(8,128)(2,1)}, bf16[24,80,128]{2,1,0:T(8,128)(2,1)}, u32[]{:S(2)}, u32[]{:S(2)}) collective-permute-start(bf16[24,80,128]{2,1,0:T(8,128)(2,1)} %get-tuple-element.16.refs_4_), channel_id=1, source_target_pairs={{0,3},{1,0},{2,1},{3,2},{4,7},{5,4},{6,5},{7,6},{8,11},{9,8},{10,9... | collective-permute-start | bytes 1474568 | tf_op jit(solution)/shard_map/ppermute | solution.py:419
  100.0 45.7 %collective-permute-start.2 = (bf16[32,64,128]{2,1,0:T(8,128)(2,1)S(1)}, bf16[32,64,128]{2,1,0:T(8,128)(2,1)S(1)}, u32[]{:S(2)}, u32[]{:S(2)}) collective-permute-start(bf16[32,64,128]{2,1,0:T(8,128)(2,1)S(1)} %collective-permute-done.refs_1_), channel_id=1, source_target_pairs={{0,1},{1,2},{2,3},{3,0},{4,5},{5,6},{6,7},{7,4},{8,9},{9,10},{10,1... | collective-permute-start | bytes 1572872 | tf_op jit(solution)/shard_map/ppermute | solution.py:420
  108.5 38.4 %collective-permute-start.5 = (bf16[32,64,128]{2,1,0:T(8,128)(2,1)}, bf16[32,64,128]{2,1,0:T(8,128)(2,1)S(1)}, u32[]{:S(2)}, u32[]{:S(2)}) collective-permute-start(bf16[32,64,128]{2,1,0:T(8,128)(2,1)} %collective-permute-done.4.refs_6_), channel_id=1, source_target_pairs={{0,3},{1,0},{2,1},{3,2},{4,7},{5,4},{6,5},{7,6},{8,11},{9,8},{10,9... | collective-permute-start | bytes 1572872 | tf_op jit(solution)/shard_map/ppermute | solution.py:420
  128.2 15.3 %copy-start.12 = (bf16[24,80,128]{2,1,0:T(8,128)(2,1)S(1)}, bf16[24,80,128]{2,1,0:T(8,128)(2,1)}, u32[]{:S(2)}) copy-start(bf16[24,80,128]{2,1,0:T(8,128)(2,1)} %get-tuple-element.15.refs_0_) | copy-start | bytes 1474564
  128.3 16.4 %copy-start.13 = (bf16[24,80,128]{2,1,0:T(8,128)(2,1)S(1)}, bf16[24,80,128]{2,1,0:T(8,128)(2,1)}, u32[]{:S(2)}) copy-start(bf16[24,80,128]{2,1,0:T(8,128)(2,1)} %get-tuple-element.16.refs_4_) | copy-start | bytes 1474564
  128.3 17.4 %copy-start.2 = (bf16[16,80,128]{2,1,0:T(8,128)(2,1)S(1)}, bf16[16,80,128]{2,1,0:T(8,128)(2,1)}, u32[]{:S(2)}) copy-start(bf16[16,80,128]{2,1,0:T(8,128)(2,1)} %get-tuple-element.17.refs_0_) | copy-start | bytes 983044
  143.6 21.0 %collective-permute-start.7 = (bf16[24,80,128]{2,1,0:T(8,128)(2,1)S(1)}, bf16[24,80,128]{2,1,0:T(8,128)(2,1)}, u32[]{:S(2)}, u32[]{:S(2)}) collective-permute-start(bf16[24,80,128]{2,1,0:T(8,128)(2,1)S(1)} %copy-done.12), channel_id=1, source_target_pairs={{0,3},{1,0},{2,1},{3,2},{4,7},{5,4},{6,5},{7,6},{8,11},{9,8},{10,9... | collective-permute-start | bytes 1474568 | tf_op jit(solution)/shard_map/ppermute | solution.py:419
  144.6 22.0 %collective-permute-start.9 = (bf16[24,80,128]{2,1,0:T(8,128)(2,1)S(1)}, bf16[24,80,128]{2,1,0:T(8,128)(2,1)}, u32[]{:S(2)}, u32[]{:S(2)}) collective-permute-start(bf16[24,80,128]{2,1,0:T(8,128)(2,1)S(1)} %copy-done.13), channel_id=1, source_target_pairs={{0,1},{1,2},{2,3},{3,0},{4,5},{5,6},{6,7},{7,4},{8,9},{9,10},{10,1... | collective-permute-start | bytes 1474568 | tf_op jit(solution)/shard_map/ppermute | solution.py:418
  145.6 48.9 %collective-permute-start.12 = (bf16[16,80,128]{2,1,0:T(8,128)(2,1)S(1)}, bf16[16,80,128]{2,1,0:T(8,128)(2,1)S(1)}, u32[]{:S(2)}, u32[]{:S(2)}) collective-permute-start(bf16[16,80,128]{2,1,0:T(8,128)(2,1)S(1)} %copy-done.2), channel_id=1, source_target_pairs={{0,1},{1,2},{2,3},{3,0},{4,5},{5,6},{6,7},{7,4},{8,9},{9,10},{10,1... | collective-permute-start | bytes 983048 | tf_op jit(solution)/shard_map/ppermute | solution.py:418
  145.7 3.2 %copy-start.10 = (bf16[32,64,128]{2,1,0:T(8,128)(2,1)}, bf16[32,64,128]{2,1,0:T(8,128)(2,1)S(1)}, u32[]{:S(2)}) copy-start(bf16[32,64,128]{2,1,0:T(8,128)(2,1)S(1)} %collective-permute-done.2.refs_3_) | copy-start | bytes 1572868
  145.7 36.3 %collective-permute-start.8 = (bf16[24,80,128]{2,1,0:T(8,128)(2,1)}, bf16[24,80,128]{2,1,0:T(8,128)(2,1)}, u32[]{:S(2)}, u32[]{:S(2)}) collective-permute-start(bf16[24,80,128]{2,1,0:T(8,128)(2,1)} %collective-permute-done.6.refs_1_), channel_id=1, source_target_pairs={{0,1},{1,2},{2,3},{3,0},{4,5},{5,6},{6,7},{7,4},{8,9},{9,10},{10,1... | collective-permute-start | bytes 1474568 | tf_op jit(solution)/shard_map/ppermute | solution.py:420
  146.9 2.1 %copy-start.11 = (bf16[32,64,128]{2,1,0:T(8,128)(2,1)}, bf16[32,64,128]{2,1,0:T(8,128)(2,1)S(1)}, u32[]{:S(2)}) copy-start(bf16[32,64,128]{2,1,0:T(8,128)(2,1)S(1)} %collective-permute-done.5.refs_7_) | copy-start | bytes 1572868
  146.9 35.2 %collective-permute-start.11 = (bf16[24,80,128]{2,1,0:T(8,128)(2,1)}, bf16[24,80,128]{2,1,0:T(8,128)(2,1)}, u32[]{:S(2)}, u32[]{:S(2)}) collective-permute-start(bf16[24,80,128]{2,1,0:T(8,128)(2,1)} %collective-permute-done.10.refs_6_), channel_id=1, source_target_pairs={{0,3},{1,0},{2,1},{3,2},{4,7},{5,4},{6,5},{7,6},{8,11},{9,8},{10,9... | collective-permute-start | bytes 1474568 | tf_op jit(solution)/shard_map/ppermute | solution.py:420
  164.6 30.0 %collective-permute-start.13 = (bf16[16,80,128]{2,1,0:T(8,128)(2,1)S(1)}, bf16[16,80,128]{2,1,0:T(8,128)(2,1)S(1)}, u32[]{:S(2)}, u32[]{:S(2)}) collective-permute-start(bf16[16,80,128]{2,1,0:T(8,128)(2,1)S(1)} %copy-done.2), channel_id=1, source_target_pairs={{0,3},{1,0},{2,1},{3,2},{4,7},{5,4},{6,5},{7,6},{8,11},{9,8},{10,9... | collective-permute-start | bytes 983048 | tf_op jit(solution)/shard_map/ppermute | solution.py:419
  166.6 28.0 %collective-permute-start.14 = (bf16[16,80,128]{2,1,0:T(8,128)(2,1)S(1)}, bf16[16,80,128]{2,1,0:T(8,128)(2,1)S(1)}, u32[]{:S(2)}, u32[]{:S(2)}) collective-permute-start(bf16[16,80,128]{2,1,0:T(8,128)(2,1)S(1)} %copy-done.2), channel_id=1, source_target_pairs={{0,2},{1,3},{2,0},{3,1},{4,6},{5,7},{6,4},{7,5},{8,10},{9,11},{10,... | collective-permute-start | bytes 983048 | tf_op jit(solution)/shard_map/ppermute | solution.py:420
  194.5 7.9 %copy-start.6 = (f32[6,8,128]{2,1,0:T(8,128)S(1)}, f32[6,8,128]{2,1,0:T(8,128)}, u32[]{:S(2)}) copy-start(f32[6,8,128]{2,1,0:T(8,128)} %shard_map.91.refs_4_) | copy-start | bytes 73732
  194.6 0.7 copy-start.3
  194.6 0.8 copy-start.4
  195.4 0.7 copy-start.5

commit v2 on v1

--- a/solution.py
+++ b/solution.py
@@ -196,38 +196,18 @@
     )(counts, inv_blocks, coupling, rhs, x_rows)
 
 
-def collect_kernel(part, chunks, st_ref, got_ref, *refs):
-    n_out = len(chunks) + (part == 0)
-    outs = refs[:n_out]
-    buf, in_sem, out_sem = refs[n_out:]
-    slots = buf.shape[0]
-
-    def copy_in(p):
-        return pltpu.make_async_copy(got_ref.at[st_ref[p]], buf.at[p], in_sem.at[p])
-
-    @pl.loop(0, slots)
-    def _(p):
-        copy_in(p).start()
-
-    made = []
+def collect_kernel(part, chunks, st_ref, got_ref, *outs):
     first = 0
     for n, (days, _) in enumerate(chunks):
-        here = slice(first * KMAX, (first + days) * KMAX)
-
-        @pl.loop(first * KMAX, (first + days) * KMAX)
-        def _(p):
-            copy_in(p).wait()
-
-        copy = pltpu.make_async_copy(buf.at[here], outs[n], out_sem.at[n])
-        copy.start()
-        made.append(copy)
-        first += days
-    if part == 0:
-        copy = pltpu.make_async_copy(buf.at[:, ROWS[0] - 16 :, :], outs[-1], out_sem.at[len(chunks)])
-        copy.start()
-        made.append(copy)
-    for copy in made:
-        copy.wait()
+
+        @pl.loop(0, days * KMAX)
+        def _(p, n=n, first=first):
+            source = st_ref[first + p]
+            outs[n][p] = got_ref[source]
+            if part == 0:
+                outs[-1][first + p] = got_ref[source, ROWS[0] - 16 :, :]
+
+        first += days * KMAX
 
 
 def collect(part, my_st, got):
@@ -236,21 +216,17 @@
     shapes = [(days * KMAX, ROWS[part], BW) for days, _ in chunks]
     if part == 0:
         shapes.append((slots, 16, BW))
-    any_spec = pl.BlockSpec(memory_space=pl.ANY)
+    vmem_spec = pl.BlockSpec(memory_space=pltpu.VMEM)
     return pl.pallas_call(
         functools.partial(collect_kernel, part, chunks),
         out_shape=tuple(jax.ShapeDtypeStruct(shape, got.dtype) for shape in shapes),
         grid_spec=pltpu.PrefetchScalarGridSpec(
             num_scalar_prefetch=1,
             grid=(1,),
-            in_specs=[any_spec],
-            out_specs=[any_spec] * len(shapes),
-            scratch_shapes=[
-                pltpu.VMEM((slots, ROWS[part], BW), got.dtype),
-                pltpu.SemaphoreType.DMA((slots,)),
-                pltpu.SemaphoreType.DMA((len(shapes),)),
-            ],
-        ),
+            in_specs=[vmem_spec],
+            out_specs=[vmem_spec] * len(shapes),
+        ),
+        compiler_params=pltpu.CompilerParams(vmem_limit_bytes=16 << 20),
         cost_estimate=pl.CostEstimate(flops=1_000_000, bytes_accessed=2_500_000, transcendentals=0),
     )(my_st, got)
 

time: 206 us -> 206 us (level)
  Pallas kernels: 82 us -> 78.9 us
  waiting for transfers between devices: 73.7 us -> 76.8 us
    ppermute x5, waiting for transfers between devices: 1.08 us -> 4.11 us  [ring(): behind = lax.ppermute(own, 'cols', perms['ahead'])]
    pallas_call x2, Pallas kernels: 6.84 us -> 3.83 us  [collect(): pl.pallas_call(functools.partial(collect_kernel, part, chunks), out_shape...]
    unnamed x34 -> x38, local copies, waits for them, and re-layouts: 7.88 us -> 8.68 us
  transfers between devices with their start and end apart: 17 -> 17, of which waited for: 5 -> 5; matrix products, arithmetic and copies ran while one was open for 2% -> 1% of each run, Pallas kernels for 35% -> 33%
where the time goes in v2:
time: 206 us; the launch traced here: 204 us
  Pallas kernels  78.9 us (38%)
  waiting for transfers between devices  76.8 us (37%)
  starting transfers between devices  34.9 us (17%)
  local copies, waits for them, and re-layouts  10.4 us (5%)
    all_to_all x2, waiting for transfers between devices, exchange(): lax.all_to_all(items.reshape(shards * ncols, ROWS[part], BW), ('days', 'c...  50.3 us
    pallas_call x3, Pallas kernels, cov_call(): pl.pallas_call(functools.partial(cov_kernel, part, lengths), out_shape=ja...  34.4 us
    pallas_call x1, Pallas kernels, gmat_call(): pl.pallas_call(gmat_kernel, out_shape=(jax.ShapeDtypeStruct((days, rows,...  16.8 us
    all_to_all x2, starting transfers between devices, exchange(): lax.all_to_all(items.reshape(shards * ncols, ROWS[part], BW), ('days', 'c...  16.2 us
    ppermute x5, waiting for transfers between devices, ring(): lax.ppermute({'ahead': behind, 'back': before, 'direct': own}[way], 'cols...  14.4 us
    pallas_call x1, Pallas kernels, solve_call(): pl.pallas_call(solve_kernel, out_shape=jax.ShapeDtypeStruct((days, groups...  13.8 us
    pallas_call x2, Pallas kernels, pack_items(): pl.pallas_call(functools.partial(pack_kernel, part, shards, day_dev), out...  10.1 us
    unnamed x38, local copies, waits for them, and re-layouts  8.68 us
  transfers between devices with their start and end apart: 17, of which 5 were waited for; matrix products, arithmetic and copies ran while one was open for 1% of the time, Pallas kernels for 33%

profile of v2, /device:TPU:0, one launch (start us, length us, event | category | flops | bytes accessed | tf_op | source)
XLA Modules:
  0.0 203.9 jit_solution(3783207949206635145)
XLA Ops:
  0.7 0.1 broadcast_in_dim.25
  0.8 0.8 copy.11
  1.6 0.7 select_reduce_fusion
  2.3 0.1 reduce_max.14
  2.4 0.7 reshape.40.st_ref
  3.1 0.6 reduce_max.18.pos_ref
  3.8 4.9 %shard_map.86 = bf16[32,4,64,128]{3,2,1,0:T(8,128)(2,1)} custom-call(s32[32]{0:T(128)} %reduce_max.18.pos_ref, s32[2048]{0:T(1024)} %reshape.40.st_ref, bf16[16384,128]{1,0:T(8,128)(2,1)} %q_ref.3, f32[1,128]{1,0:T(1,128)} %bitcast.28), custom_call_target="tpu_custom_call" | custom-call | flops 5000000 | bytes 5000000 | tf_op jit(solution)/shard_map/pallas_call | solution.py:88
  8.7 11.4 %all-to-all-start = ((bf16[128,64,128]{2,1,0:T(8,128)(2,1)}), bf16[128,64,128]{2,1,0:T(8,128)(2,1)S(1)}, u32[]{:S(2)}, u32[]{:S(2)}) async-start(bf16[128,64,128]{2,1,0:T(8,128)(2,1)} %bitcast.22), calls=%async_computation | async-start | bytes 4194304 | tf_op jit(solution)/shard_map/all_to_all | solution.py:383
  20.1 5.2 %shard_map.89 = bf16[32,4,80,128]{3,2,1,0:T(8,128)(2,1)} custom-call(s32[32]{0:T(128)} %reduce_max.18.pos_ref, s32[2048]{0:T(1024)} %reshape.40.st_ref, bf16[16384,128]{1,0:T(8,128)(2,1)} %q_ref.3, f32[1,128]{1,0:T(1,128)} %bitcast.29), custom_call_target="tpu_custom_call" | custom-call | flops 5000000 | bytes 5000000 | tf_op jit(solution)/shard_map/pallas_call | solution.py:88
  25.3 24.8 %all-to-all-done.got_ref = bf16[128,64,128]{2,1,0:T(8,128)(2,1)S(1)} async-done(((bf16[128,64,128]{2,1,0:T(8,128)(2,1)}), bf16[128,64,128]{2,1,0:T(8,128)(2,1)S(1)}, u32[]{:S(2)}, u32[]{:S(2)}) %all-to-all-start) | async-done | bytes 2097184 | tf_op jit(solution)/shard_map/all_to_all | solution.py:383
  50.1 1.4 copy-done
  51.5 4.8 %all-to-all-start.1 = ((bf16[128,80,128]{2,1,0:T(8,128)(2,1)}), bf16[128,80,128]{2,1,0:T(8,128)(2,1)S(1)}, u32[]{:S(2)}, u32[]{:S(2)}) async-start(bf16[128,80,128]{2,1,0:T(8,128)(2,1)} %bitcast.21), calls=%async_computation.1 | async-start | bytes 5242880 | tf_op jit(solution)/shard_map/all_to_all | solution.py:383
  56.3 0.1 constant_dynamic-slice_fusion
  56.4 0.1 copy.10
  56.4 0.1 reshape.39.st_ref
  56.5 1.6 copy-done.1
  58.1 1.8 shard_map.87
  59.9 0.7 copy-done.3
  60.6 0.8 collective-permute-start
  61.4 2.4 %collective-permute-start.1 = (bf16[32,64,128]{2,1,0:T(8,128)(2,1)S(1)}, bf16[32,64,128]{2,1,0:T(8,128)(2,1)}, u32[]{:S(2)}, u32[]{:S(2)}) collective-permute-start(bf16[32,64,128]{2,1,0:T(8,128)(2,1)S(1)} %get-tuple-element.13.refs_0_), channel_id=1, source_target_pairs={{0,3},{1,0},{2,1},{3,2},{4,7},{5,4},{6,5},{7,6},{8,11},{9,8},{10,9... | collective-permute-start | bytes 1572872 | tf_op jit(solution)/shard_map/ppermute | solution.py:395
  63.8 0.9 collective-permute-start.4
  64.7 0.6 dynamic_slice.6.cnt_ref
  65.3 1.2 collective-permute-start.3
  66.4 25.5 %all-to-all-done.1.got_ref = bf16[128,80,128]{2,1,0:T(8,128)(2,1)S(1)} async-done(((bf16[128,80,128]{2,1,0:T(8,128)(2,1)}), bf16[128,80,128]{2,1,0:T(8,128)(2,1)S(1)}, u32[]{:S(2)}, u32[]{:S(2)}) %all-to-all-start.1) | async-done | bytes 2621472 | tf_op jit(solution)/shard_map/all_to_all | solution.py:383
  91.9 2.0 shard_map.90
  94.0 0.6 collective-permute-start.6
  94.5 4.1 %collective-permute-done.refs_1_ = bf16[32,64,128]{2,1,0:T(8,128)(2,1)} collective-permute-done((bf16[32,64,128]{2,1,0:T(8,128)(2,1)S(1)}, bf16[32,64,128]{2,1,0:T(8,128)(2,1)}, u32[]{:S(2)}, u32[]{:S(2)}) %collective-permute-start) | collective-permute-done | bytes 524320 | tf_op jit(solution)/shard_map/ppermute | solution.py:394
  98.6 0.8 collective-permute-start.10
  99.5 0.0 collective-permute-done.1.refs_2_
  99.5 1.2 collective-permute-start.2
  100.7 8.0 %collective-permute-done.4.refs_6_ = bf16[32,64,128]{2,1,0:T(8,128)(2,1)} collective-permute-done((bf16[32,64,128]{2,1,0:T(8,128)(2,1)}, bf16[32,64,128]{2,1,0:T(8,128)(2,1)}, u32[]{:S(2)}, u32[]{:S(2)}) %collective-permute-start.4) | collective-permute-done | bytes 524320 | tf_op jit(solution)/shard_map/ppermute | solution.py:395
  108.6 2.3 %collective-permute-start.5 = (bf16[32,64,128]{2,1,0:T(8,128)(2,1)}, bf16[32,64,128]{2,1,0:T(8,128)(2,1)S(1)}, u32[]{:S(2)}, u32[]{:S(2)}) collective-permute-start(bf16[32,64,128]{2,1,0:T(8,128)(2,1)} %collective-permute-done.4.refs_6_), channel_id=1, source_target_pairs={{0,3},{1,0},{2,1},{3,2},{4,7},{5,4},{6,5},{7,6},{8,11},{9,8},{10,9... | collective-permute-start | bytes 1572872 | tf_op jit(solution)/shard_map/ppermute | solution.py:396
  110.9 16.8 %gmat.1 = (bf16[8,1024,1024]{2,1,0:T(8,128)(2,1)}, f32[8,8,128]{2,1,0:T(8,128)}) custom-call(s32[8]{0:T(128)} %dynamic_slice.6.cnt_ref, bf16[8,1024,128]{2,1,0:T(8,128)(2,1)} %inv_ref.3, bf16[8,1024,1024]{2,1,0:T(8,128)(2,1)} %coup_ref.3), custom_call_target="tpu_custom_call" | custom-call | flops 8589934592 | bytes 33554432 | tf_op jit(solution)/shard_map/gmat/pallas_call | solution.py:128
  127.7 0.0 copy-done.10
  127.7 0.6 copy.20
  128.3 13.8 %solve.1 = f32[8,8,128]{2,1,0:T(8,128)} custom-call(s32[8]{0:T(128)} %dynamic_slice.6.cnt_ref, bf16[8,1024,128]{2,1,0:T(8,128)(2,1)} %inv_ref.3, bf16[8,1024,1024]{2,1,0:T(8,128)(2,1)} %coup_ref.3, f32[8,8,128]{2,1,0:T(8,128)} %bitcast.23, bf16[8,8,16,128]{3,2,1,0:T(8,128)(2,1)} %bitcast.20), custom_call_target="tpu_custom_call" | custom-call | flops 4294967296 | bytes 16777216 | tf_op jit(solution)/shard_map/solve/pallas_call | solution.py:178
  142.1 1.4 copy.19
  143.5 0.0 collective-permute-done.3.refs_5_
  143.5 1.0 collective-permute-start.7
  144.5 0.0 collective-permute-done.6.refs_1_
  144.5 1.0 collective-permute-start.9
  145.5 0.0 collective-permute-done.10.refs_6_
  145.5 0.1 collective-permute-start.12
  145.6 0.0 collective-permute-done.2.refs_3_
  145.6 1.2 collective-permute-start.8
  146.8 0.0 collective-permute-done.5.refs_7_
  146.8 2.0 %collective-permute-start.11 = (bf16[24,80,128]{2,1,0:T(8,128)(2,1)S(1)}, bf16[24,80,128]{2,1,0:T(8,128)(2,1)}, u32[]{:S(2)}, u32[]{:S(2)}) collective-permute-start(bf16[24,80,128]{2,1,0:T(8,128)(2,1)S(1)} %collective-permute-done.10.refs_6_), channel_id=1, source_target_pairs={{0,3},{1,0},{2,1},{3,2},{4,7},{5,4},{6,5},{7,6},{8,11},{9,8},{10,9... | collective-permute-start | bytes 1474568 | tf_op jit(solution)/shard_map/ppermute | solution.py:396
  148.9 15.6 %shard_map.88.base_ref.refs_8_ = f32[8,8,128]{2,1,0:T(8,128)} custom-call(s32[1]{0:T(128)} %bitcast.3.me_ref, bf16[8,1024,1024]{2,1,0:T(8,128)(2,1)} %get-tuple-element.11.g_ref, f32[8,8,128]{2,1,0:T(8,128)} %get-tuple-element.12.base_ref.refs_8_, bf16[32,64,128]{2,1,0:T(8,128)(2,1)} %copy-done.4, bf16[32,64,128]{2,1,0:T(8,128)(2,1)} %collective-permute-done.refs_1_, ...), custom_call_target="tpu_custom_call" | custom-call | flops 6442450944 | bytes 16777216 | tf_op jit(solution)/shard_map/pallas_call | solution.py:332
  164.5 0.0 collective-permute-done.7.refs_2_
  164.6 2.0 collective-permute-start.13
  166.6 0.0 collective-permute-done.9.refs_5_
  166.6 1.3 collective-permute-start.14
  167.8 14.4 %collective-permute-done.8.refs_3_ = bf16[24,80,128]{2,1,0:T(8,128)(2,1)} collective-permute-done((bf16[24,80,128]{2,1,0:T(8,128)(2,1)S(1)}, bf16[24,80,128]{2,1,0:T(8,128)(2,1)}, u32[]{:S(2)}, u32[]{:S(2)}) %collective-permute-start.8) | collective-permute-done | bytes 491552 | tf_op jit(solution)/shard_map/ppermute | solution.py:396
  182.2 0.0 collective-permute-done.11.refs_7_
  182.2 12.5 %shard_map.91.refs_4_ = f32[6,8,128]{2,1,0:T(8,128)} custom-call(s32[1]{0:T(128)} %bitcast.3.me_ref, bf16[8,1024,1024]{2,1,0:T(8,128)(2,1)} %get-tuple-element.11.g_ref, f32[8,8,128]{2,1,0:T(8,128)} %shard_map.88.base_ref.refs_8_, bf16[24,80,128]{2,1,0:T(8,128)(2,1)} %get-tuple-element.15.refs_0_, bf16[24,80,128]{2,1,0:T(8,128)(2,1)} %copy-done.13, ...), custom_call_target="tpu_custom_call" | custom-call | flops 6442450944 | bytes 12582912 | tf_op jit(solution)/shard_map/pallas_call | solution.py:332
  194.7 0.0 collective-permute-done.12.refs_1_
  194.7 0.0 collective-permute-done.13.refs_2_
  194.8 0.0 collective-permute-done.14.refs_3_
  194.8 0.7 copy-done.5
  195.5 0.1 copy-done.6
  195.6 0.7 copy-done.7
  196.3 6.3 %shard_map.92 = f32[2,8,128]{2,1,0:T(8,128)} custom-call(s32[1]{0:T(128)} %bitcast.3.me_ref, bf16[8,1024,1024]{2,1,0:T(8,128)(2,1)} %get-tuple-element.11.g_ref, f32[8,8,128]{2,1,0:T(8,128)} %shard_map.88.base_ref.refs_8_, bf16[16,80,128]{2,1,0:T(8,128)(2,1)} %copy-done.2, bf16[16,80,128]{2,1,0:T(8,128)(2,1)} %copy-done.5, bf16[16,80,128]{2,1,0:T(8,128)(2,1)} %copy-done.6, ...), custom_call_target="tpu_custom_call" | custom-call | flops 2147483648 | bytes 4194304 | tf_op jit(solution)/shard_map/pallas_call | solution.py:332
  202.6 0.7 maximum_bitcast_fusion
  203.3 0.6 copy.18
  (29 shorter events, 0.1 us)
Async XLA Ops:
  8.7 41.4 %all-to-all-start = ((bf16[128,64,128]{2,1,0:T(8,128)(2,1)}), bf16[128,64,128]{2,1,0:T(8,128)(2,1)S(1)}, u32[]{:S(2)}, u32[]{:S(2)}) async-start(bf16[128,64,128]{2,1,0:T(8,128)(2,1)} %bitcast.22), calls=%async_computation | async-start | bytes 4194304 | tf_op jit(solution)/shard_map/all_to_all | solution.py:383
  50.1 1.4 copy-start
  51.5 4.8 %copy-start.9 = (s32[256,8]{0,1:T(8,128)S(1)}, s32[256,8]{0,1:T(8,128)}, u32[]{:S(2)}) copy-start(s32[256,8]{0,1:T(8,128)} %param.7) | copy-start | bytes 24580
  51.5 13.2 %copy-start.16 = (s32[256]{0:T(256)S(1)}, s32[256]{0:T(256)}, u32[]{:S(2)}) copy-start(s32[256]{0:T(256)} %param.8) | copy-start | bytes 3076
  51.5 40.5 %all-to-all-start.1 = ((bf16[128,80,128]{2,1,0:T(8,128)(2,1)}), bf16[128,80,128]{2,1,0:T(8,128)(2,1)S(1)}, u32[]{:S(2)}, u32[]{:S(2)}) async-start(bf16[128,80,128]{2,1,0:T(8,128)(2,1)} %bitcast.21), calls=%async_computation.1 | async-start | bytes 5242880 | tf_op jit(solution)/shard_map/all_to_all | solution.py:383
  56.5 1.6 copy-start.1
  59.9 0.7 copy-start.3
  60.6 67.1 %copy-start.4 = (bf16[32,64,128]{2,1,0:T(8,128)(2,1)}, bf16[32,64,128]{2,1,0:T(8,128)(2,1)S(1)}, u32[]{:S(2)}) copy-start(bf16[32,64,128]{2,1,0:T(8,128)(2,1)S(1)} %get-tuple-element.13.refs_0_) | copy-start | bytes 1572868
  60.6 38.0 %collective-permute-start = (bf16[32,64,128]{2,1,0:T(8,128)(2,1)S(1)}, bf16[32,64,128]{2,1,0:T(8,128)(2,1)}, u32[]{:S(2)}, u32[]{:S(2)}) collective-permute-start(bf16[32,64,128]{2,1,0:T(8,128)(2,1)S(1)} %get-tuple-element.13.refs_0_), channel_id=1, source_target_pairs={{0,1},{1,2},{2,3},{3,0},{4,5},{5,6},{6,7},{7,4},{8,9},{9,10},{10,1... | collective-permute-start | bytes 1572872 | tf_op jit(solution)/shard_map/ppermute | solution.py:394
  61.4 38.1 %collective-permute-start.1 = (bf16[32,64,128]{2,1,0:T(8,128)(2,1)S(1)}, bf16[32,64,128]{2,1,0:T(8,128)(2,1)}, u32[]{:S(2)}, u32[]{:S(2)}) collective-permute-start(bf16[32,64,128]{2,1,0:T(8,128)(2,1)S(1)} %get-tuple-element.13.refs_0_), channel_id=1, source_target_pairs={{0,3},{1,0},{2,1},{3,2},{4,7},{5,4},{6,5},{7,6},{8,11},{9,8},{10,9... | collective-permute-start | bytes 1572872 | tf_op jit(solution)/shard_map/ppermute | solution.py:395
  63.8 44.8 %collective-permute-start.4 = (bf16[32,64,128]{2,1,0:T(8,128)(2,1)}, bf16[32,64,128]{2,1,0:T(8,128)(2,1)}, u32[]{:S(2)}, u32[]{:S(2)}) collective-permute-start(bf16[32,64,128]{2,1,0:T(8,128)(2,1)} %get-tuple-element.14.refs_4_), channel_id=1, source_target_pairs={{0,3},{1,0},{2,1},{3,2},{4,7},{5,4},{6,5},{7,6},{8,11},{9,8},{10,9... | collective-permute-start | bytes 1572872 | tf_op jit(solution)/shard_map/ppermute | solution.py:395
  65.3 78.2 %collective-permute-start.3 = (bf16[32,64,128]{2,1,0:T(8,128)(2,1)}, bf16[32,64,128]{2,1,0:T(8,128)(2,1)}, u32[]{:S(2)}, u32[]{:S(2)}) collective-permute-start(bf16[32,64,128]{2,1,0:T(8,128)(2,1)} %get-tuple-element.14.refs_4_), channel_id=1, source_target_pairs={{0,1},{1,2},{2,3},{3,0},{4,5},{5,6},{6,7},{7,4},{8,9},{9,10},{10,1... | collective-permute-start | bytes 1572872 | tf_op jit(solution)/shard_map/ppermute | solution.py:394
  94.0 72.6 %copy-start.2 = (bf16[16,80,128]{2,1,0:T(8,128)(2,1)}, bf16[16,80,128]{2,1,0:T(8,128)(2,1)S(1)}, u32[]{:S(2)}) copy-start(bf16[16,80,128]{2,1,0:T(8,128)(2,1)S(1)} %get-tuple-element.17.refs_0_) | copy-start | bytes 983044
  94.0 50.6 %collective-permute-start.6 = (bf16[24,80,128]{2,1,0:T(8,128)(2,1)}, bf16[24,80,128]{2,1,0:T(8,128)(2,1)S(1)}, u32[]{:S(2)}, u32[]{:S(2)}) collective-permute-start(bf16[24,80,128]{2,1,0:T(8,128)(2,1)} %get-tuple-element.15.refs_0_), channel_id=1, source_target_pairs={{0,1},{1,2},{2,3},{3,0},{4,5},{5,6},{6,7},{7,4},{8,9},{9,10},{10,1... | collective-permute-start | bytes 1474568 | tf_op jit(solution)/shard_map/ppermute | solution.py:394
  98.6 29.0 %copy-start.10 = (f32[8,1024]{1,0:T(8,128)S(1)}, f32[8,1024]{1,0:T(8,128)}, u32[]{:S(2)}) copy-start(f32[8,1024]{1,0:T(8,128)} %param.13) | copy-start | bytes 98308
  98.6 46.9 %collective-permute-start.10 = (bf16[24,80,128]{2,1,0:T(8,128)(2,1)}, bf16[24,80,128]{2,1,0:T(8,128)(2,1)S(1)}, u32[]{:S(2)}, u32[]{:S(2)}) collective-permute-start(bf16[24,80,128]{2,1,0:T(8,128)(2,1)} %get-tuple-element.16.refs_4_), channel_id=1, source_target_pairs={{0,3},{1,0},{2,1},{3,2},{4,7},{5,4},{6,5},{7,6},{8,11},{9,8},{10,9... | collective-permute-start | bytes 1474568 | tf_op jit(solution)/shard_map/ppermute | solution.py:395
  99.5 46.1 %collective-permute-start.2 = (bf16[32,64,128]{2,1,0:T(8,128)(2,1)}, bf16[32,64,128]{2,1,0:T(8,128)(2,1)S(1)}, u32[]{:S(2)}, u32[]{:S(2)}) collective-permute-start(bf16[32,64,128]{2,1,0:T(8,128)(2,1)} %collective-permute-done.refs_1_), channel_id=1, source_target_pairs={{0,1},{1,2},{2,3},{3,0},{4,5},{5,6},{6,7},{7,4},{8,9},{9,10},{10,1... | collective-permute-start | bytes 1572872 | tf_op jit(solution)/shard_map/ppermute | solution.py:396
  108.6 38.2 %collective-permute-start.5 = (bf16[32,64,128]{2,1,0:T(8,128)(2,1)}, bf16[32,64,128]{2,1,0:T(8,128)(2,1)S(1)}, u32[]{:S(2)}, u32[]{:S(2)}) collective-permute-start(bf16[32,64,128]{2,1,0:T(8,128)(2,1)} %collective-permute-done.4.refs_6_), channel_id=1, source_target_pairs={{0,3},{1,0},{2,1},{3,2},{4,7},{5,4},{6,5},{7,6},{8,11},{9,8},{10,9... | collective-permute-start | bytes 1572872 | tf_op jit(solution)/shard_map/ppermute | solution.py:396
  143.5 21.0 %collective-permute-start.7 = (bf16[24,80,128]{2,1,0:T(8,128)(2,1)}, bf16[24,80,128]{2,1,0:T(8,128)(2,1)S(1)}, u32[]{:S(2)}, u32[]{:S(2)}) collective-permute-start(bf16[24,80,128]{2,1,0:T(8,128)(2,1)} %get-tuple-element.15.refs_0_), channel_id=1, source_target_pairs={{0,3},{1,0},{2,1},{3,2},{4,7},{5,4},{6,5},{7,6},{8,11},{9,8},{10,9... | collective-permute-start | bytes 1474568 | tf_op jit(solution)/shard_map/ppermute | solution.py:395
  144.5 20.0 %copy-start.13 = (bf16[24,80,128]{2,1,0:T(8,128)(2,1)}, bf16[24,80,128]{2,1,0:T(8,128)(2,1)S(1)}, u32[]{:S(2)}) copy-start(bf16[24,80,128]{2,1,0:T(8,128)(2,1)S(1)} %collective-permute-done.6.refs_1_) | copy-start | bytes 1474564
  144.5 22.0 %collective-permute-start.9 = (bf16[24,80,128]{2,1,0:T(8,128)(2,1)}, bf16[24,80,128]{2,1,0:T(8,128)(2,1)}, u32[]{:S(2)}, u32[]{:S(2)}) collective-permute-start(bf16[24,80,128]{2,1,0:T(8,128)(2,1)} %get-tuple-element.16.refs_4_), channel_id=1, source_target_pairs={{0,1},{1,2},{2,3},{3,0},{4,5},{5,6},{6,7},{7,4},{8,9},{9,10},{10,1... | collective-permute-start | bytes 1474568 | tf_op jit(solution)/shard_map/ppermute | solution.py:394
  145.5 19.0 %copy-start.14 = (bf16[24,80,128]{2,1,0:T(8,128)(2,1)}, bf16[24,80,128]{2,1,0:T(8,128)(2,1)S(1)}, u32[]{:S(2)}) copy-start(bf16[24,80,128]{2,1,0:T(8,128)(2,1)S(1)} %collective-permute-done.10.refs_6_) | copy-start | bytes 1474564
  145.5 49.2 %collective-permute-start.12 = (bf16[16,80,128]{2,1,0:T(8,128)(2,1)S(1)}, bf16[16,80,128]{2,1,0:T(8,128)(2,1)S(1)}, u32[]{:S(2)}, u32[]{:S(2)}) collective-permute-start(bf16[16,80,128]{2,1,0:T(8,128)(2,1)S(1)} %get-tuple-element.17.refs_0_), channel_id=1, source_target_pairs={{0,1},{1,2},{2,3},{3,0},{4,5},{5,6},{6,7},{7,4},{8,9},{9,10},{10,1... | collective-permute-start | bytes 983048 | tf_op jit(solution)/shard_map/ppermute | solution.py:394
  145.6 3.2 %copy-start.11 = (bf16[32,64,128]{2,1,0:T(8,128)(2,1)}, bf16[32,64,128]{2,1,0:T(8,128)(2,1)S(1)}, u32[]{:S(2)}) copy-start(bf16[32,64,128]{2,1,0:T(8,128)(2,1)S(1)} %collective-permute-done.2.refs_3_) | copy-start | bytes 1572868
  145.6 36.6 %collective-permute-start.8 = (bf16[24,80,128]{2,1,0:T(8,128)(2,1)S(1)}, bf16[24,80,128]{2,1,0:T(8,128)(2,1)}, u32[]{:S(2)}, u32[]{:S(2)}) collective-permute-start(bf16[24,80,128]{2,1,0:T(8,128)(2,1)S(1)} %collective-permute-done.6.refs_1_), channel_id=1, source_target_pairs={{0,1},{1,2},{2,3},{3,0},{4,5},{5,6},{6,7},{7,4},{8,9},{9,10},{10,1... | collective-permute-start | bytes 1474568 | tf_op jit(solution)/shard_map/ppermute | solution.py:396
  146.8 2.1 %copy-start.12 = (bf16[32,64,128]{2,1,0:T(8,128)(2,1)}, bf16[32,64,128]{2,1,0:T(8,128)(2,1)S(1)}, u32[]{:S(2)}) copy-start(bf16[32,64,128]{2,1,0:T(8,128)(2,1)S(1)} %collective-permute-done.5.refs_7_) | copy-start | bytes 1572868
  146.8 35.4 %collective-permute-start.11 = (bf16[24,80,128]{2,1,0:T(8,128)(2,1)S(1)}, bf16[24,80,128]{2,1,0:T(8,128)(2,1)}, u32[]{:S(2)}, u32[]{:S(2)}) collective-permute-start(bf16[24,80,128]{2,1,0:T(8,128)(2,1)S(1)} %collective-permute-done.10.refs_6_), channel_id=1, source_target_pairs={{0,3},{1,0},{2,1},{3,2},{4,7},{5,4},{6,5},{7,6},{8,11},{9,8},{10,9... | collective-permute-start | bytes 1474568 | tf_op jit(solution)/shard_map/ppermute | solution.py:396
  164.5 17.7 %copy-start.15 = (bf16[24,80,128]{2,1,0:T(8,128)(2,1)}, bf16[24,80,128]{2,1,0:T(8,128)(2,1)S(1)}, u32[]{:S(2)}) copy-start(bf16[24,80,128]{2,1,0:T(8,128)(2,1)S(1)} %collective-permute-done.7.refs_2_) | copy-start | bytes 1474564
  164.6 30.2 %collective-permute-start.13 = (bf16[16,80,128]{2,1,0:T(8,128)(2,1)S(1)}, bf16[16,80,128]{2,1,0:T(8,128)(2,1)S(1)}, u32[]{:S(2)}, u32[]{:S(2)}) collective-permute-start(bf16[16,80,128]{2,1,0:T(8,128)(2,1)S(1)} %get-tuple-element.17.refs_0_), channel_id=1, source_target_pairs={{0,3},{1,0},{2,1},{3,2},{4,7},{5,4},{6,5},{7,6},{8,11},{9,8},{10,9... | collective-permute-start | bytes 983048 | tf_op jit(solution)/shard_map/ppermute | solution.py:395
  166.6 28.2 %collective-permute-start.14 = (bf16[16,80,128]{2,1,0:T(8,128)(2,1)S(1)}, bf16[16,80,128]{2,1,0:T(8,128)(2,1)S(1)}, u32[]{:S(2)}, u32[]{:S(2)}) collective-permute-start(bf16[16,80,128]{2,1,0:T(8,128)(2,1)S(1)} %get-tuple-element.17.refs_0_), channel_id=1, source_target_pairs={{0,2},{1,3},{2,0},{3,1},{4,6},{5,7},{6,4},{7,5},{8,10},{9,11},{10,... | collective-permute-start | bytes 983048 | tf_op jit(solution)/shard_map/ppermute | solution.py:396
  194.7 7.9 %copy-start.8 = (f32[6,8,128]{2,1,0:T(8,128)S(1)}, f32[6,8,128]{2,1,0:T(8,128)}, u32[]{:S(2)}) copy-start(f32[6,8,128]{2,1,0:T(8,128)} %shard_map.91.refs_4_) | copy-start | bytes 73732
  194.7 0.7 copy-start.5
  194.7 0.8 copy-start.6
  195.6 0.7 copy-start.7
